TPU v7x, 32 devices: a whole 2x2x4 slice. The times are simulated.
32 devices in a mesh: dp: 8 (over z, x), mp: 4 (over y, core).
Axes of the slice: x: 2, y: 2, z: 4, core: 2. Of those that a mesh axis runs over, the one named last changes fastest.
Arguments:
- q_latent: bfloat16 [2048, 2, 768], P('dp', None, 'mp'), may hold values from -6 to 6
- kv_latent: bfloat16 [2048, 2, 256], P('dp', None, 'mp'), may hold values from -6 to 6
- q_head_grad: bfloat16 [2048, 512], P('dp'), may hold values from -0.1875 to 0.1875
- k_head_grad: bfloat16 [2048, 512], P('dp'), may hold values from -0.1875 to 0.1875
- q_heads: bfloat16 [2048, 512], P('dp', 'mp'), may hold values from -6 to 6
- k_heads: bfloat16 [2048, 512], P('dp', 'mp'), may hold values from -6 to 6
- query_pick: int32 [8, 16, 4], P('dp', None, 'mp'), may hold values from 0 to 255
- key_pick: int32 [8, 16, 4], P('dp', None, 'mp'), may hold values from 0 to 255
- q_weight: float32 [8, 768, 128], P('dp', 'mp'), may hold values from -6 to 6
- k_weight: float32 [8, 256, 128], P('dp', 'mp'), may hold values from -6 to 6
- q_moment: float32 [8, 768, 128], P('dp', 'mp'), may hold values from -6 to 6
- k_moment: float32 [8, 256, 128], P('dp', 'mp'), may hold values from -6 to 6
Outputs:
- q_weight_new: float32 [8, 768, 128], P('dp', 'mp')
- k_weight_new: float32 [8, 256, 128], P('dp', 'mp')
- q_moment_new: float32 [8, 768, 128], P('dp', 'mp')
- k_moment_new: float32 [8, 256, 128], P('dp', 'mp')
Inputs may be any that keep to these rules, and one draw needn't show every extreme that they name: `query_pick`: the index of a token among the 256 tokens of its own block b. `key_pick`: the index of a token among the 256 tokens of its own block b.
All inputs are finite; a program needn't handle non-finite values.
Results may differ from a plain program's by a relative error of at most 0.0003.
Values sent between devices are 32-bit elements; how exact they have to be, the bound alone decides.
A program may use at most 64 MiB of HBM per device.

v0:
```python
import functools
import math

import jax
import jax.numpy as jnp
from jax import lax
from jax.experimental import pallas as pl
from jax.experimental.pallas import tpu as pltpu
from jax.sharding import PartitionSpec as P

ITERS = 5
MOMENTUM = 0.95
STEP_SIZE = 1.0
DECAY = 0.1
CLIP_LEVEL = 0.1
SCORE_SCALE = 1.0 / math.sqrt(192.0)
COEFF_A = 3.4445
COEFF_B = -4.775
COEFF_C = 2.0315
LOWEST = -1e30
MESH = pl.DeviceIdType.MESH
F32 = jnp.float32
BF16 = jnp.bfloat16


def split(value):
    high = value.astype(BF16)
    return high, (value - high.astype(F32)).astype(BF16)


def mm(a, b):
    return jnp.dot(a, b, preferred_element_type=F32)


def mm3(a, b):
    both = mm(a[0], jnp.concatenate([b[0], b[1]], axis=1))
    width = b[0].shape[1]
    return both[:, :width] + (both[:, width:] + mm(a[1], b[0]))


def gram(rows):
    high, low = split(rows)
    high_t = high.T
    cross = mm(high_t, low)
    return mm(high_t, high) + (cross + cross.T)


def fold(matrix):
    width = matrix.shape[0]
    half = width // 2
    row = lax.broadcasted_iota(jnp.int32, (half, width), 0)
    lane = lax.broadcasted_iota(jnp.int32, (half, width), 1)
    lower = matrix[half:]
    body = jnp.where(lane >= row, matrix[:half], pltpu.roll(lower, half, 1))
    ends = jnp.sum(jnp.where(lane == row + half, lower, 0.0), axis=0, keepdims=True)
    return body, jnp.broadcast_to(ends, (8, width))


def unfold(message):
    width = message.shape[1]
    half = width // 2
    row = lax.broadcasted_iota(jnp.int32, (half, width), 0)
    lane = lax.broadcasted_iota(jnp.int32, (half, width), 1)
    body = message[:half]
    ends = jnp.broadcast_to(message[half : half + 1], (half, width))
    top = jnp.where(lane >= row, body, 0.0)
    strict = jnp.where((lane >= half) & (lane - half < row), pltpu.roll(body, half, 1), 0.0)
    one_side = jnp.concatenate([top, jnp.where(lane == row + half, ends, strict)], axis=0)
    full_row = lax.broadcasted_iota(jnp.int32, (width, width), 0)
    full_lane = lax.broadcasted_iota(jnp.int32, (width, width), 1)
    return one_side + jnp.where(full_row == full_lane, 0.0, one_side.T)


def column(row):
    count = row.shape[1]
    spread = jnp.broadcast_to(row, (count, count))
    same = lax.broadcasted_iota(jnp.int32, (count, count), 0) == lax.broadcasted_iota(
        jnp.int32, (count, count), 1
    )
    picked = jnp.where(same, spread, 0).astype(F32)
    return jnp.sum(picked, axis=1, keepdims=True).astype(jnp.int32)


def partner(index, count, step):
    if count & (count - 1):
        return lax.rem(index + step, count)
    result = 0
    bit = 1
    while bit < count:
        held = lax.rem(lax.div(index, bit), 2)
        result = result + bit * ((1 - held) if step & bit else held)
        bit *= 2
    return result


def kernel(
    n_dp, n_mp, heads,
    ql_in, kl_in, qg_in, kg_in, qh_in, kh_in, qp_in, kp_in, qw_in, kw_in, qm_in, km_in,
    qw_out, kw_out, qm_out, km_out, mix, shrink_out,
    ql_ref, kl_ref, qg_ref, kg_ref, qh_ref, kh_ref, qp_ref, kp_ref, qw_ref, kw_ref, qm_ref, km_ref, in_sems,
    near_send, near_recv, own, far_recv, peak_send, peak_recv, peak2_send, peak2_recv,
    grams, gram_recv, row_send, row_recv,
    ns_s, ns_r, fs_s, fs_r, pk_s, pk_r, pm_s, pm_r, g_s, g_r, y_s, y_r, m_s, m_r,
):
    dp = lax.axis_index("dp")
    mp = lax.axis_index("mp")
    n_outer = n_dp // 2
    outer = lax.div(dp, 2)
    inner = lax.rem(dp, 2)
    core = lax.rem(mp, 2)
    group = lax.div(mp, 2)
    n_group = n_mp // 2
    q_rows = qm_ref.shape[1]
    k_rows = km_ref.shape[1]
    width = qm_ref.shape[2]
    tokens = qg_ref.shape[0]
    other_core = mp + 1 - 2 * core

    loads = [
        pltpu.make_async_copy(src, dst, in_sems.at[i])
        for i, (src, dst) in enumerate((
            (ql_in, ql_ref), (kl_in, kl_ref), (qg_in, qg_ref), (kg_in, kg_ref),
            (qp_in, qp_ref), (kp_in, kp_ref), (qh_in, qh_ref), (kh_in, kh_ref),
            (qm_in, qm_ref), (km_in, km_ref), (qw_in, qw_ref), (kw_in, kw_ref),
        ))
    ]
    for each in loads:
        each.start()

    barrier = pltpu.get_barrier_semaphore()
    for step in range(1, n_dp):
        pl.semaphore_signal(
            barrier, inc=1, device_id=(lax.rem(dp + step, n_dp), mp), device_id_type=MESH
        )
    def owner(step):
        across = lax.rem(dp + (step // n_group) * heads, n_dp)
        return across, 2 * lax.rem(group + step, n_group) + core

    for step in range(n_group + 1, 2 * n_group):
        pl.semaphore_signal(barrier, inc=1, device_id=owner(step), device_id_type=MESH)
    for step in range(1, n_mp):
        pl.semaphore_signal(
            barrier, inc=1, device_id=(dp, lax.rem(mp + step, n_mp)), device_id_type=MESH
        )

    def copy(src, dst, send, recv, where):
        return pltpu.make_async_remote_copy(
            src_ref=src, dst_ref=dst, send_sem=send, recv_sem=recv,
            device_id=where, device_id_type=MESH,
        )

    def term(dst, where, to_outer, to_inner):
        slot = 2 * to_outer + to_inner
        half = lax.div(slot, heads)
        cols = pl.ds(pl.multiple_of(lax.rem(slot, heads) * width, width), width)
        dst[where, :q_rows, :] = mm(ql_ref[half], qg_ref[:, cols])
        dst[where, q_rows:, :] = mm(kl_ref[half], kg_ref[:, cols])

    for each in loads[:4]:
        each.wait()
    order = list(range(n_outer - 1, -1, -1))
    neighbour = (dp + 1 - 2 * inner, mp)
    near = []
    for spot, step in enumerate(order):
        term(near_send, spot, partner(outer, n_outer, step), 1 - inner)
        if spot == 0:
            pl.semaphore_wait(barrier, n_dp + n_mp + n_group - 3)
        each = copy(near_send.at[spot], near_recv.at[spot], ns_s.at[spot], ns_r.at[spot], neighbour)
        each.start()
        near.append(each)

    for each in loads[4:8]:
        each.wait()
    local_heads = qp_ref.shape[0]
    lane = lax.broadcasted_iota(jnp.int32, (8, width), 1)
    peaks = jnp.full((8, width), LOWEST, F32)
    ids = lax.broadcasted_iota(jnp.int32, (qp_ref.shape[2], tokens), 1)
    for head in range(local_heads):
        span = slice(head * width, (head + 1) * width)
        pick_q = (ids == column(qp_ref[head])).astype(F32).astype(BF16)
        pick_k = (ids == column(kp_ref[head])).astype(F32).astype(BF16)
        score = jnp.sum(
            mm(pick_q, qh_ref[:, span]) * mm(pick_k, kh_ref[:, span]), axis=1, keepdims=True
        )
        top = jnp.max(score * SCORE_SCALE, axis=0, keepdims=True)
        peaks = jnp.where(lane == mp * local_heads + head, top, peaks)
    peak_send[...] = peaks
    peak_copies = []
    for step in range(1, n_dp):
        each = copy(
            peak_send, peak_recv.at[step - 1], pk_s.at[step - 1], pk_r.at[step - 1],
            (lax.rem(dp + step, n_dp), mp),
        )
        each.start()
        peak_copies.append(each)

    for spot, step in enumerate(order):
        term(own, spot, partner(outer, n_outer, step), inner)
    last = n_outer - 1
    relayed = n_outer == 4
    inside = lax.rem(lax.div(outer, 2) + lax.rem(outer, 2), 2)
    far = []
    for spot, step in enumerate(order):
        near[spot].wait_recv()
        if not step:
            continue
        own[spot] = own[spot] + near_recv[spot]
        where = spot
        target = partner(outer, n_outer, step)
        if relayed and spot == 0:
            where = last * (1 - inside)
            aside = partner(outer, n_outer, 1)
            target = aside + inside * (target - aside)
        if relayed and spot == 1:

            @pl.when(inside == 1)
            def _():
                copy(
                    own.at[0], far_recv.at[last], fs_s.at[0], fs_r.at[last], (dp, mp)
                ).wait_recv()
                own[1] = own[1] + far_recv[last]

        each = copy(
            own.at[spot], far_recv.at[where], fs_s.at[spot], fs_r.at[where],
            (2 * target + inner, mp),
        )
        each.start()
        far.append(each)
    own[last] = own[last] + near_recv[last]

    for each in peak_copies:
        each.wait_recv()
    peaks = jnp.maximum(peaks, jnp.max(peak_recv[...], axis=0))
    peak2_send[...] = peaks
    peak2_copies = []
    for step in range(1, n_mp):
        each = copy(
            peak2_send, peak2_recv.at[step - 1], pm_s.at[step - 1], pm_r.at[step - 1],
            (dp, lax.rem(mp + step, n_mp)),
        )
        each.start()
        peak2_copies.append(each)

    if relayed:

        @pl.when(inside == 1)
        def _():
            copy(own.at[0], far_recv.at[0], fs_s.at[0], fs_r.at[0], (dp, mp)).wait_recv()
            own[last] = own[last] + far_recv[0]

    total = own[last]
    for spot in range(1 if relayed else 0, last):
        far[spot].wait_recv()
        total = total + far_recv[spot]
    for each in loads[8:]:
        each.wait()
    q_moment = MOMENTUM * qm_ref[0] + total[:q_rows]
    k_moment = MOMENTUM * km_ref[0] + total[q_rows:]
    qm_out[0] = q_moment
    km_out[0] = k_moment

    top = width // 2
    for which, matrix in enumerate((gram(q_moment), gram(k_moment))):
        body, ends = fold(matrix)
        grams[which, :top, :] = body
        grams[which, top:, :] = ends
    swap = copy(grams.at[1 - core], gram_recv, g_s, g_r, (dp, other_core))
    swap.start()
    swap.wait_recv()
    whole = grams[core] + gram_recv[...]
    row_send[...] = whole
    rows = []
    for step in range(1, 2 * n_group):
        each = copy(
            row_send, row_recv.at[step - 1], y_s.at[step - 1], y_r.at[step - 1], owner(step)
        )
        each.start()
        rows.append(each)
    for each in peak2_copies:
        each.wait_recv()
    peaks = jnp.maximum(peaks, jnp.max(peak2_recv[...], axis=0))
    mine = jnp.where(lane == lax.rem(dp, heads), peaks, LOWEST)
    peak = jnp.max(jnp.max(mine, axis=0, keepdims=True), axis=1, keepdims=True)
    shrink = jnp.sqrt(CLIP_LEVEL / jnp.maximum(peak, CLIP_LEVEL))
    keep = 1.0 - STEP_SIZE * DECAY
    shrink_out[...] = jnp.broadcast_to(shrink, shrink_out.shape)
    qw_out[0] = (qw_ref[0] * keep) * shrink
    kw_out[0] = (kw_ref[0] * keep) * shrink
    for each in rows:
        each.wait_recv()
    whole = unfold(whole + jnp.sum(row_recv[...], axis=0))

    eye = (
        lax.broadcasted_iota(jnp.int32, (width, width), 0)
        == lax.broadcasted_iota(jnp.int32, (width, width), 1)
    ).astype(F32)
    trace = jnp.sum(jnp.sum(whole * eye, axis=0, keepdims=True), axis=1, keepdims=True)
    scale = 1.0 / jnp.sqrt(trace + 1.0)
    current = whole * (scale * scale)
    mixed = None
    for step in range(ITERS):
        parts = split(current)
        square = mm3(parts, parts)
        poly = COEFF_A * eye + COEFF_B * current + COEFF_C * square
        pair = split(poly)
        mixed = poly * scale if mixed is None else mm3(split(mixed), pair)
        if step + 1 < ITERS:
            current = mm3(split(mm3(parts, pair)), pair)
    mix[core] = mixed
    swap2 = copy(mix.at[core], mix.at[core], m_s, m_r, (dp, other_core))
    swap2.start()

    swap2.wait_recv()
    for each in near + far + peak_copies + peak2_copies + [swap] + rows + [swap2]:
        each.wait_send()


def finish(n_mp, qw_ref, kw_ref, qm_ref, km_ref, mix_ref, shrink_ref, qw_out, kw_out, qm_out, km_out):
    groups = ((qw_ref, qm_ref, qw_out, qm_out), (kw_ref, km_ref, kw_out, km_out))
    for which, (weight, moment, weight_out, moment_out) in enumerate(groups):
        rows = moment[0]
        size = STEP_SIZE * 0.2 * math.sqrt(2 * n_mp * rows.shape[0])
        ortho = mm3(split(rows), split(mix_ref[which]))
        moment_out[0] = rows
        weight_out[0] = weight[0] - (size * ortho) * shrink_ref[0:1, :]


def local(
    q_latent, kv_latent, q_head_grad, k_head_grad, q_heads, k_heads,
    query_pick, key_pick, q_weight, k_weight, q_moment, k_moment,
):
    n_dp = lax.axis_size("dp")
    n_mp = lax.axis_size("mp")
    heads = n_dp // 2
    n_outer = n_dp // 2
    n_group = n_mp // 2
    rows = q_latent.shape[2] + kv_latent.shape[2]
    width = q_moment.shape[2]
    operands = (
        q_latent.transpose(1, 2, 0), kv_latent.transpose(1, 2, 0), q_head_grad, k_head_grad,
        q_heads, k_heads, query_pick.transpose(2, 0, 1), key_pick.transpose(2, 0, 1),
        q_weight, k_weight, q_moment, k_moment,
    )
    vmem = pltpu.VMEM
    dma = pltpu.SemaphoreType.DMA
    square = (width, width)
    folded = (width // 2 + 8, width)
    tile = (8, width)
    shapes = [a.shape for a in (q_weight, k_weight, q_moment, k_moment)]
    parts = pl.pallas_call(
        functools.partial(kernel, n_dp, n_mp, heads),
        out_shape=[vmem(shape, F32) for shape in shapes + [(2,) + square, tile]],
        in_specs=[pl.BlockSpec(memory_space=pl.ANY)] * 12,
        out_specs=[pl.BlockSpec(memory_space=vmem)] * 6,
        scratch_shapes=[vmem(a.shape, a.dtype) for a in operands] + [
            dma((12,)),
            vmem((n_outer, rows, width), F32),
            vmem((n_outer, rows, width), F32),
            vmem((n_outer, rows, width), F32),
            vmem((n_outer, rows, width), F32),
            vmem(tile, F32),
            vmem((n_dp - 1,) + tile, F32),
            vmem(tile, F32),
            vmem((n_mp - 1,) + tile, F32),
            vmem((2,) + folded, F32),
            vmem(folded, F32),
            vmem(folded, F32),
            vmem((2 * n_group - 1,) + folded, F32),
            dma((n_outer,)), dma((n_outer,)),
            dma((n_outer,)), dma((n_outer,)),
            dma((n_dp - 1,)), dma((n_dp - 1,)),
            dma((n_mp - 1,)), dma((n_mp - 1,)),
            dma, dma,
            dma((2 * n_group - 1,)), dma((2 * n_group - 1,)),
            dma, dma,
        ],
        compiler_params=pltpu.CompilerParams(
            collective_id=0, has_side_effects=True, vmem_limit_bytes=56 * 1024 * 1024
        ),
    )(*operands)
    return pl.pallas_call(
        functools.partial(finish, n_mp),
        out_shape=[jax.ShapeDtypeStruct(shape, F32) for shape in shapes],
        in_specs=[pl.BlockSpec(memory_space=vmem)] * 6,
        out_specs=[pl.BlockSpec(memory_space=vmem)] * 4,
    )(*[pltpu.with_memory_space_constraint(part, vmem) for part in parts])


def solution(mesh):
    rows3 = P("dp", "mp", None)
    in_specs = (
        P("dp", None, "mp"), P("dp", None, "mp"), P("dp", None), P("dp", None),
        P("dp", "mp"), P("dp", "mp"), P("dp", None, "mp"), P("dp", None, "mp"),
        rows3, rows3, rows3, rows3,
    )
    return jax.shard_map(
        lambda *args: tuple(local(*args)),
        mesh=mesh, in_specs=in_specs, out_specs=(rows3,) * 4, check_vma=False,
    )
```

profile of v0, /device:TPU:0, one launch (start us, length us, event | category | flops | bytes accessed | tf_op | source)
XLA Modules:
  0.0 31.8 jit_solution(15580580390361723205)
XLA Ops:
  0.6 30.3 %shard_map.147 = (f32[1,192,128]{2,1,0:T(8,128)S(1)}, f32[1,64,128]{2,1,0:T(8,128)S(1)}, f32[1,192,128]{2,1,0:T(8,128)S(1)}, f32[1,64,128]{2,1,0:T(8,128)S(1)}, ...) custom-call(bf16[2,192,256]{2,1,0:T(8,128)(2,1)} %bitcast.4, bf16[2,64,256]{2,1,0:T(8,128)(2,1)} %bitcast.5, ...), custom_call_target="tpu_custom_call" | custom-call | tf_op jit(solution)/shard_map/pallas_call | solution.py:350
  30.9 0.9 %shard_map.148 = (f32[1,192,128]{2,1,0:T(8,128)}, f32[1,64,128]{2,1,0:T(8,128)}, f32[1,192,128]{2,1,0:T(8,128)}, f32[1,64,128]{2,1,0:T(8,128)}) custom-call(f32[1,192,128]{2,1,0:T(8,128)S(1)} %get-tuple-element.10.qw_ref, f32[1,64,128]{2,1,0:T(8,128)S(1)} %get-tuple-element.11.kw_ref, f32[1,192,128]{2,1,0:T(8,128)S(1)} %get-tuple-element.12.qm_ref, ...), custom_call_target="tpu_custom_call" | custom-call | tf_op jit(solution)/shard_map/pallas_call | solution.py:381
where the time goes:
time: 32 us; the launch traced here: 31.8 us
  Pallas kernels  31.2 us (98%)
  between operations  0.64 us (2%)
    pallas_call x1, Pallas kernels, local(): pl.pallas_call(functools.partial(kernel, n_dp, n_mp, heads), out_shape=[v...  30.3 us
    pallas_call x1, Pallas kernels, local(): pl.pallas_call(functools.partial(finish, n_mp), out_shape=[jax.ShapeDtype...  0.9 us

commit v1 on v0

--- a/solution.py
+++ b/solution.py
@@ -9,6 +9,7 @@
 from jax.sharding import PartitionSpec as P
 
 ITERS = 5
+CHUNKS = 4
 MOMENTUM = 0.95
 STEP_SIZE = 1.0
 DECAY = 0.1
@@ -98,9 +99,9 @@
     ql_in, kl_in, qg_in, kg_in, qh_in, kh_in, qp_in, kp_in, qw_in, kw_in, qm_in, km_in,
     qw_out, kw_out, qm_out, km_out, mix, shrink_out,
     ql_ref, kl_ref, qg_ref, kg_ref, qh_ref, kh_ref, qp_ref, kp_ref, qw_ref, kw_ref, qm_ref, km_ref, in_sems,
-    near_send, near_recv, own, far_recv, peak_send, peak_recv, peak2_send, peak2_recv,
+    near_send, near_recv, own, far_recv, raw_recv, peak_send, peak_recv, peak2_send, peak2_recv,
     grams, gram_recv, row_send, row_recv,
-    ns_s, ns_r, fs_s, fs_r, pk_s, pk_r, pm_s, pm_r, g_s, g_r, y_s, y_r, m_s, m_r,
+    ns_s, ns_r, fs_s, fs_r, rw_s, rw_r, pk_s, pk_r, pm_s, pm_r, g_s, g_r, y_s, y_r, m_s, m_r,
 ):
     dp = lax.axis_index("dp")
     mp = lax.axis_index("mp")
@@ -158,16 +159,75 @@
 
     for each in loads[:4]:
         each.wait()
-    order = list(range(n_outer - 1, -1, -1))
+    entered = n_dp + n_mp + n_group - 3
     neighbour = (dp + 1 - 2 * inner, mp)
-    near = []
-    for spot, step in enumerate(order):
-        term(near_send, spot, partner(outer, n_outer, step), 1 - inner)
-        if spot == 0:
-            pl.semaphore_wait(barrier, n_dp + n_mp + n_group - 3)
-        each = copy(near_send.at[spot], near_recv.at[spot], ns_s.at[spot], ns_r.at[spot], neighbour)
+    last = n_outer - 1
+    line = n_outer == 4
+    tall = q_rows + k_rows
+    step_rows = tall // CHUNKS
+    half = tall // 2
+    inside = lax.rem(lax.div(outer, 2) + lax.rem(outer, 2), 2)
+    by = [partner(outer, n_outer, step) for step in range(n_outer)]
+
+    def rows_of(chunk):
+        return pl.ds(chunk * step_rows, step_rows)
+
+    if line:
+        split_to = by[2] + inside * (by[1] - by[2])
+        whole_to = by[1] + inside * (by[2] - by[1])
+        order = [by[3], split_to, whole_to, by[0]]
+        spans = [range(CHUNKS), range(CHUNKS // 2), range(CHUNKS), range(CHUNKS)]
+    else:
+        order = by[::-1]
+        spans = [range(CHUNKS)] * n_outer
+
+    def near_copy(spot, chunk):
+        where = rows_of(chunk)
+        return copy(
+            near_send.at[spot, where], near_recv.at[spot, where],
+            ns_s.at[spot, chunk], ns_r.at[spot, chunk], neighbour,
+        )
+
+    def far_copy(spot, slot, chunk, target):
+        where = rows_of(chunk)
+        return copy(
+            own.at[spot, where], far_recv.at[slot, where],
+            fs_s.at[spot, chunk], fs_r.at[slot, chunk], (2 * target + inner, mp),
+        )
+
+    def raw_copy(which):
+        source = (near_send, own)[which]
+        return copy(
+            source.at[1, pl.ds(half, half)], raw_recv.at[which],
+            rw_s.at[which], rw_r.at[which], (2 * split_to + inner, mp),
+        )
+
+    near, far, raw = [], [], []
+
+    def start(into, each):
         each.start()
-        near.append(each)
+        into.append(each)
+
+    term(near_send, 0, order[0], 1 - inner)
+    pl.semaphore_wait(barrier, entered)
+    for chunk in spans[0]:
+        start(near, near_copy(0, chunk))
+    if line:
+        term(near_send, 1, order[1], 1 - inner)
+        start(raw, raw_copy(0))
+        for chunk in spans[1]:
+            start(near, near_copy(1, chunk))
+        term(own, 1, order[1], inner)
+        start(raw, raw_copy(1))
+    for spot in range(2 if line else 1, n_outer):
+        term(near_send, spot, order[spot], 1 - inner)
+        for chunk in spans[spot]:
+            if line and spot == last and chunk >= CHUNKS // 2:
+                continue
+            start(near, near_copy(spot, chunk))
+    for spot in range(n_outer):
+        if not (line and spot == 1):
+            term(own, spot, order[spot], inner)
 
     for each in loads[4:8]:
         each.wait()
@@ -194,39 +254,44 @@
         each.start()
         peak_copies.append(each)
 
-    for spot, step in enumerate(order):
-        term(own, spot, partner(outer, n_outer, step), inner)
-    last = n_outer - 1
-    relayed = n_outer == 4
-    inside = lax.rem(lax.div(outer, 2) + lax.rem(outer, 2), 2)
-    far = []
-    for spot, step in enumerate(order):
-        near[spot].wait_recv()
-        if not step:
-            continue
-        own[spot] = own[spot] + near_recv[spot]
-        where = spot
-        target = partner(outer, n_outer, step)
-        if relayed and spot == 0:
-            where = last * (1 - inside)
-            aside = partner(outer, n_outer, 1)
-            target = aside + inside * (target - aside)
-        if relayed and spot == 1:
+    def meet(spot, chunk):
+        near_copy(spot, chunk).wait_recv()
+        where = rows_of(chunk)
+        own[spot, where] = own[spot, where] + near_recv[spot, where]
+
+    def gather(slot, chunk):
+        far_copy(0, slot, chunk, outer).wait_recv()
+        return far_recv[slot, rows_of(chunk)]
+
+    relay = 3
+    if line:
+        first_to = by[1] + inside * (by[3] - by[1])
+        for chunk in spans[0]:
+            meet(0, chunk)
+            start(far, far_copy(0, relay * (1 - inside), chunk, first_to))
+        raw[0].wait_recv()
+        low = pl.ds(half, half)
+        near_send[last, low] = near_send[last, low] + raw_recv[0]
+        for chunk in range(CHUNKS // 2, CHUNKS):
+            start(near, near_copy(last, chunk))
+        for chunk in spans[1]:
+            meet(1, chunk)
+            start(far, far_copy(1, 1, chunk, split_to))
+        raw[1].wait_recv()
+        own[last, low] = own[last, low] + raw_recv[1]
+        for chunk in spans[2]:
 
             @pl.when(inside == 1)
             def _():
-                copy(
-                    own.at[0], far_recv.at[last], fs_s.at[0], fs_r.at[last], (dp, mp)
-                ).wait_recv()
-                own[1] = own[1] + far_recv[last]
-
-        each = copy(
-            own.at[spot], far_recv.at[where], fs_s.at[spot], fs_r.at[where],
-            (2 * target + inner, mp),
-        )
-        each.start()
-        far.append(each)
-    own[last] = own[last] + near_recv[last]
+                own[2, rows_of(chunk)] = own[2, rows_of(chunk)] + gather(relay, chunk)
+
+            meet(2, chunk)
+            start(far, far_copy(2, 2, chunk, whole_to))
+    else:
+        for spot in range(last):
+            for chunk in spans[spot]:
+                meet(spot, chunk)
+                start(far, far_copy(spot, spot, chunk, order[spot]))
 
     for each in peak_copies:
         each.wait_recv()
@@ -241,17 +306,24 @@
         each.start()
         peak2_copies.append(each)
 
-    if relayed:
+    if line:
 
         @pl.when(inside == 1)
         def _():
-            copy(own.at[0], far_recv.at[0], fs_s.at[0], fs_r.at[0], (dp, mp)).wait_recv()
-            own[last] = own[last] + far_recv[0]
-
+            for chunk in spans[0]:
+                own[last, rows_of(chunk)] = own[last, rows_of(chunk)] + gather(0, chunk)
+
+        for chunk in spans[1]:
+            own[last, rows_of(chunk)] = own[last, rows_of(chunk)] + gather(1, chunk)
+        for chunk in spans[last]:
+            meet(last, chunk)
+            own[last, rows_of(chunk)] = own[last, rows_of(chunk)] + gather(2, chunk)
+    else:
+        for chunk in spans[last]:
+            meet(last, chunk)
+            for spot in range(last):
+                own[last, rows_of(chunk)] = own[last, rows_of(chunk)] + gather(spot, chunk)
     total = own[last]
-    for spot in range(1 if relayed else 0, last):
-        far[spot].wait_recv()
-        total = total + far_recv[spot]
     for each in loads[8:]:
         each.wait()
     q_moment = MOMENTUM * qm_ref[0] + total[:q_rows]
@@ -311,7 +383,7 @@
     swap2.start()
 
     swap2.wait_recv()
-    for each in near + far + peak_copies + peak2_copies + [swap] + rows + [swap2]:
+    for each in near + far + raw + peak_copies + peak2_copies + [swap] + rows + [swap2]:
         each.wait_send()
 
 
@@ -358,6 +430,7 @@
             vmem((n_outer, rows, width), F32),
             vmem((n_outer, rows, width), F32),
             vmem((n_outer, rows, width), F32),
+            vmem((2, rows // 2, width), F32),
             vmem(tile, F32),
             vmem((n_dp - 1,) + tile, F32),
             vmem(tile, F32),
@@ -366,8 +439,9 @@
             vmem(folded, F32),
             vmem(folded, F32),
             vmem((2 * n_group - 1,) + folded, F32),
-            dma((n_outer,)), dma((n_outer,)),
-            dma((n_outer,)), dma((n_outer,)),
+            dma((n_outer, CHUNKS)), dma((n_outer, CHUNKS)),
+            dma((n_outer, CHUNKS)), dma((n_outer, CHUNKS)),
+            dma((2,)), dma((2,)),
             dma((n_dp - 1,)), dma((n_dp - 1,)),
             dma((n_mp - 1,)), dma((n_mp - 1,)),
             dma, dma,

time: 32 us -> 30.2 us (0.944)
  the two profiles are of different devices: /device:TPU:0 before, /device:TPU:9 now
where the time goes in v1:
time: 30.2 us; the launch traced here: 30.1 us
  Pallas kernels  29.4 us (97%)
  between operations  0.64 us (2%)
    pallas_call x1, Pallas kernels, local(): pl.pallas_call(functools.partial(kernel, n_dp, n_mp, heads), out_shape=[v...  28.5 us
    pallas_call x1, Pallas kernels, local(): pl.pallas_call(functools.partial(finish, n_mp), out_shape=[jax.ShapeDtype...  0.9 us

profile of v1, /device:TPU:9, one launch (start us, length us, event | category | flops | bytes accessed | tf_op | source)
XLA Modules:
  0.0 30.1 jit_solution(7890914650326974979)
XLA Ops:
  0.6 28.5 %shard_map.147 = (f32[1,192,128]{2,1,0:T(8,128)S(1)}, f32[1,64,128]{2,1,0:T(8,128)S(1)}, f32[1,192,128]{2,1,0:T(8,128)S(1)}, f32[1,64,128]{2,1,0:T(8,128)S(1)}, ...) custom-call(bf16[2,192,256]{2,1,0:T(8,128)(2,1)} %bitcast.4, bf16[2,64,256]{2,1,0:T(8,128)(2,1)} %bitcast.5, ...), custom_call_target="tpu_custom_call" | custom-call | tf_op jit(solution)/shard_map/pallas_call | solution.py:422
  29.2 0.9 %shard_map.148 = (f32[1,192,128]{2,1,0:T(8,128)}, f32[1,64,128]{2,1,0:T(8,128)}, f32[1,192,128]{2,1,0:T(8,128)}, f32[1,64,128]{2,1,0:T(8,128)}) custom-call(f32[1,192,128]{2,1,0:T(8,128)S(1)} %get-tuple-element.10.qw_ref, f32[1,64,128]{2,1,0:T(8,128)S(1)} %get-tuple-element.11.kw_ref, f32[1,192,128]{2,1,0:T(8,128)S(1)} %get-tuple-element.12.qm_ref, ...), custom_call_target="tpu_custom_call" | custom-call | tf_op jit(solution)/shard_map/pallas_call | solution.py:455

commit v2 on v1

--- a/solution.py
+++ b/solution.py
@@ -9,7 +9,6 @@
 from jax.sharding import PartitionSpec as P
 
 ITERS = 5
-CHUNKS = 4
 MOMENTUM = 0.95
 STEP_SIZE = 1.0
 DECAY = 0.1
@@ -39,11 +38,15 @@
     return both[:, :width] + (both[:, width:] + mm(a[1], b[0]))
 
 
-def gram(rows):
+def gram_pair(rows):
     high, low = split(rows)
-    high_t = high.T
-    cross = mm(high_t, low)
-    return mm(high_t, high) + (cross + cross.T)
+    return mm(high.T, jnp.concatenate([high, low], axis=1))
+
+
+def gram_of(pair):
+    width = pair.shape[0]
+    cross = pair[:, width:]
+    return pair[:, :width] + (cross + cross.T)
 
 
 def fold(matrix):
@@ -54,7 +57,7 @@
     lower = matrix[half:]
     body = jnp.where(lane >= row, matrix[:half], pltpu.roll(lower, half, 1))
     ends = jnp.sum(jnp.where(lane == row + half, lower, 0.0), axis=0, keepdims=True)
-    return body, jnp.broadcast_to(ends, (8, width))
+    return jnp.concatenate([body, ends], axis=0)
 
 
 def unfold(message):
@@ -154,8 +157,8 @@
         slot = 2 * to_outer + to_inner
         half = lax.div(slot, heads)
         cols = pl.ds(pl.multiple_of(lax.rem(slot, heads) * width, width), width)
-        dst[where, :q_rows, :] = mm(ql_ref[half], qg_ref[:, cols])
-        dst[where, q_rows:, :] = mm(kl_ref[half], kg_ref[:, cols])
+        dst[where, :k_rows, :] = mm(kl_ref[half], kg_ref[:, cols])
+        dst[where, k_rows:, :] = mm(ql_ref[half], qg_ref[:, cols])
 
     for each in loads[:4]:
         each.wait()
@@ -164,7 +167,8 @@
     last = n_outer - 1
     line = n_outer == 4
     tall = q_rows + k_rows
-    step_rows = tall // CHUNKS
+    step_rows = k_rows
+    chunks = tall // step_rows
     half = tall // 2
     inside = lax.rem(lax.div(outer, 2) + lax.rem(outer, 2), 2)
     by = [partner(outer, n_outer, step) for step in range(n_outer)]
@@ -176,10 +180,11 @@
         split_to = by[2] + inside * (by[1] - by[2])
         whole_to = by[1] + inside * (by[2] - by[1])
         order = [by[3], split_to, whole_to, by[0]]
-        spans = [range(CHUNKS), range(CHUNKS // 2), range(CHUNKS), range(CHUNKS)]
+        kept = chunks // 2
+        spans = [range(chunks), range(kept), range(chunks), range(chunks)]
     else:
         order = by[::-1]
-        spans = [range(CHUNKS)] * n_outer
+        spans = [range(chunks)] * n_outer
 
     def near_copy(spot, chunk):
         where = rows_of(chunk)
@@ -202,38 +207,36 @@
             rw_s.at[which], rw_r.at[which], (2 * split_to + inner, mp),
         )
 
-    near, far, raw = [], [], []
-
-    def start(into, each):
-        each.start()
-        into.append(each)
-
+    def send_near(spot, which):
+        for chunk in which:
+            near_copy(spot, chunk).start()
+
+    raw = [raw_copy(0), raw_copy(1)] if line else []
     term(near_send, 0, order[0], 1 - inner)
     pl.semaphore_wait(barrier, entered)
-    for chunk in spans[0]:
-        start(near, near_copy(0, chunk))
+    send_near(0, spans[0])
     if line:
         term(near_send, 1, order[1], 1 - inner)
-        start(raw, raw_copy(0))
-        for chunk in spans[1]:
-            start(near, near_copy(1, chunk))
+        raw[0].start()
         term(own, 1, order[1], inner)
-        start(raw, raw_copy(1))
-    for spot in range(2 if line else 1, n_outer):
-        term(near_send, spot, order[spot], 1 - inner)
-        for chunk in spans[spot]:
-            if line and spot == last and chunk >= CHUNKS // 2:
-                continue
-            start(near, near_copy(spot, chunk))
-    for spot in range(n_outer):
-        if not (line and spot == 1):
-            term(own, spot, order[spot], inner)
+        raw[1].start()
+        term(near_send, 2, order[2], 1 - inner)
+
+        @pl.when(inside == 1)
+        def _():
+            send_near(2, spans[2])
+            send_near(1, spans[1])
+
+        @pl.when(inside == 0)
+        def _():
+            send_near(1, spans[1])
+            send_near(2, spans[2])
 
     for each in loads[4:8]:
         each.wait()
     local_heads = qp_ref.shape[0]
-    lane = lax.broadcasted_iota(jnp.int32, (8, width), 1)
-    peaks = jnp.full((8, width), LOWEST, F32)
+    lane = lax.broadcasted_iota(jnp.int32, (1, width), 1)
+    peaks = jnp.full((1, width), LOWEST, F32)
     ids = lax.broadcasted_iota(jnp.int32, (qp_ref.shape[2], tokens), 1)
     for head in range(local_heads):
         span = slice(head * width, (head + 1) * width)
@@ -254,6 +257,17 @@
         each.start()
         peak_copies.append(each)
 
+    if line:
+        term(near_send, last, order[last], 1 - inner)
+        send_near(last, range(kept))
+    else:
+        for spot in range(1, n_outer):
+            term(near_send, spot, order[spot], 1 - inner)
+            send_near(spot, spans[spot])
+    for spot in range(n_outer):
+        if not (line and spot == 1):
+            term(own, spot, order[spot], inner)
+
     def meet(spot, chunk):
         near_copy(spot, chunk).wait_recv()
         where = rows_of(chunk)
@@ -264,35 +278,92 @@
         return far_recv[slot, rows_of(chunk)]
 
     relay = 3
+
+    def pass_on(spot):
+        for chunk in spans[spot]:
+            meet(spot, chunk)
+            far_copy(spot, spot, chunk, order[spot]).start()
+
     if line:
         first_to = by[1] + inside * (by[3] - by[1])
         for chunk in spans[0]:
             meet(0, chunk)
-            start(far, far_copy(0, relay * (1 - inside), chunk, first_to))
+            far_copy(0, relay * (1 - inside), chunk, first_to).start()
         raw[0].wait_recv()
         low = pl.ds(half, half)
         near_send[last, low] = near_send[last, low] + raw_recv[0]
-        for chunk in range(CHUNKS // 2, CHUNKS):
-            start(near, near_copy(last, chunk))
-        for chunk in spans[1]:
-            meet(1, chunk)
-            start(far, far_copy(1, 1, chunk, split_to))
+        send_near(last, range(kept, chunks))
+
+        @pl.when(inside == 1)
+        def _():
+            for chunk in spans[2]:
+                own[2, rows_of(chunk)] = own[2, rows_of(chunk)] + gather(relay, chunk)
+                meet(2, chunk)
+                far_copy(2, 2, chunk, whole_to).start()
+            pass_on(1)
+            for chunk in spans[0]:
+                own[last, rows_of(chunk)] = own[last, rows_of(chunk)] + gather(0, chunk)
+
+        @pl.when(inside == 0)
+        def _():
+            pass_on(1)
+            pass_on(2)
+
         raw[1].wait_recv()
         own[last, low] = own[last, low] + raw_recv[1]
-        for chunk in spans[2]:
-
-            @pl.when(inside == 1)
-            def _():
-                own[2, rows_of(chunk)] = own[2, rows_of(chunk)] + gather(relay, chunk)
-
-            meet(2, chunk)
-            start(far, far_copy(2, 2, chunk, whole_to))
     else:
         for spot in range(last):
-            for chunk in spans[spot]:
-                meet(spot, chunk)
-                start(far, far_copy(spot, spot, chunk, order[spot]))
-
+            pass_on(spot)
+
+    for each in loads[8:]:
+        each.wait()
+
+    def complete(chunk):
+        where = rows_of(chunk)
+        meet(last, chunk)
+        if line:
+            if chunk in spans[1]:
+                own[last, where] = own[last, where] + gather(1, chunk)
+            total = own[last, where] + gather(2, chunk)
+        else:
+            total = own[last, where]
+            for spot in range(last):
+                total = total + gather(spot, chunk)
+        if not chunk:
+            rows = MOMENTUM * km_ref[0] + total
+            km_out[0] = rows
+        else:
+            part = pl.ds((chunk - 1) * step_rows, step_rows)
+            rows = MOMENTUM * qm_ref[0, part] + total
+            qm_out[0, part] = rows
+        return gram_pair(rows)
+
+    swap = copy(grams.at[1 - core], gram_recv, g_s, g_r, (dp, other_core))
+    grams[1] = fold(gram_of(complete(0)))
+
+    @pl.when(core == 0)
+    def _():
+        swap.start()
+
+    pair = complete(1)
+    for chunk in range(2, chunks):
+        pair = pair + complete(chunk)
+    grams[0] = fold(gram_of(pair))
+
+    @pl.when(core == 1)
+    def _():
+        swap.start()
+
+    swap.wait_recv()
+    whole = grams[core] + gram_recv[...]
+    row_send[...] = whole
+    rows = []
+    for step in range(1, 2 * n_group):
+        each = copy(
+            row_send, row_recv.at[step - 1], y_s.at[step - 1], y_r.at[step - 1], owner(step)
+        )
+        each.start()
+        rows.append(each)
     for each in peak_copies:
         each.wait_recv()
     peaks = jnp.maximum(peaks, jnp.max(peak_recv[...], axis=0))
@@ -306,58 +377,6 @@
         each.start()
         peak2_copies.append(each)
 
-    if line:
-
-        @pl.when(inside == 1)
-        def _():
-            for chunk in spans[0]:
-                own[last, rows_of(chunk)] = own[last, rows_of(chunk)] + gather(0, chunk)
-
-        for chunk in spans[1]:
-            own[last, rows_of(chunk)] = own[last, rows_of(chunk)] + gather(1, chunk)
-        for chunk in spans[last]:
-            meet(last, chunk)
-            own[last, rows_of(chunk)] = own[last, rows_of(chunk)] + gather(2, chunk)
-    else:
-        for chunk in spans[last]:
-            meet(last, chunk)
-            for spot in range(last):
-                own[last, rows_of(chunk)] = own[last, rows_of(chunk)] + gather(spot, chunk)
-    total = own[last]
-    for each in loads[8:]:
-        each.wait()
-    q_moment = MOMENTUM * qm_ref[0] + total[:q_rows]
-    k_moment = MOMENTUM * km_ref[0] + total[q_rows:]
-    qm_out[0] = q_moment
-    km_out[0] = k_moment
-
-    top = width // 2
-    for which, matrix in enumerate((gram(q_moment), gram(k_moment))):
-        body, ends = fold(matrix)
-        grams[which, :top, :] = body
-        grams[which, top:, :] = ends
-    swap = copy(grams.at[1 - core], gram_recv, g_s, g_r, (dp, other_core))
-    swap.start()
-    swap.wait_recv()
-    whole = grams[core] + gram_recv[...]
-    row_send[...] = whole
-    rows = []
-    for step in range(1, 2 * n_group):
-        each = copy(
-            row_send, row_recv.at[step - 1], y_s.at[step - 1], y_r.at[step - 1], owner(step)
-        )
-        each.start()
-        rows.append(each)
-    for each in peak2_copies:
-        each.wait_recv()
-    peaks = jnp.maximum(peaks, jnp.max(peak2_recv[...], axis=0))
-    mine = jnp.where(lane == lax.rem(dp, heads), peaks, LOWEST)
-    peak = jnp.max(jnp.max(mine, axis=0, keepdims=True), axis=1, keepdims=True)
-    shrink = jnp.sqrt(CLIP_LEVEL / jnp.maximum(peak, CLIP_LEVEL))
-    keep = 1.0 - STEP_SIZE * DECAY
-    shrink_out[...] = jnp.broadcast_to(shrink, shrink_out.shape)
-    qw_out[0] = (qw_ref[0] * keep) * shrink
-    kw_out[0] = (kw_ref[0] * keep) * shrink
     for each in rows:
         each.wait_recv()
     whole = unfold(whole + jnp.sum(row_recv[...], axis=0))
@@ -381,9 +400,23 @@
     mix[core] = mixed
     swap2 = copy(mix.at[core], mix.at[core], m_s, m_r, (dp, other_core))
     swap2.start()
-
+    for each in peak2_copies:
+        each.wait_recv()
+    peaks = jnp.maximum(peaks, jnp.max(peak2_recv[...], axis=0))
+    mine = jnp.where(lane == lax.rem(dp, heads), peaks, LOWEST)
+    peak = jnp.max(jnp.max(mine, axis=0, keepdims=True), axis=1, keepdims=True)
+    shrink = jnp.sqrt(CLIP_LEVEL / jnp.maximum(peak, CLIP_LEVEL))
+    keep = 1.0 - STEP_SIZE * DECAY
+    shrink_out[...] = jnp.broadcast_to(shrink, shrink_out.shape)
+    qw_out[0] = (qw_ref[0] * keep) * shrink
+    kw_out[0] = (kw_ref[0] * keep) * shrink
     swap2.wait_recv()
-    for each in near + far + raw + peak_copies + peak2_copies + [swap] + rows + [swap2]:
+    for spot in range(n_outer):
+        for chunk in spans[spot]:
+            near_copy(spot, chunk).wait_send()
+            if spot < last:
+                far_copy(spot, spot, chunk, order[spot]).wait_send()
+    for each in raw + peak_copies + peak2_copies + [swap] + rows + [swap2]:
         each.wait_send()
 
 
@@ -394,7 +427,7 @@
         size = STEP_SIZE * 0.2 * math.sqrt(2 * n_mp * rows.shape[0])
         ortho = mm3(split(rows), split(mix_ref[which]))
         moment_out[0] = rows
-        weight_out[0] = weight[0] - (size * ortho) * shrink_ref[0:1, :]
+        weight_out[0] = weight[0] - (size * ortho) * shrink_ref[...]
 
 
 def local(
@@ -416,8 +449,9 @@
     vmem = pltpu.VMEM
     dma = pltpu.SemaphoreType.DMA
     square = (width, width)
-    folded = (width // 2 + 8, width)
-    tile = (8, width)
+    folded = (width // 2 + 1, width)
+    tile = (1, width)
+    chunks = rows // k_moment.shape[1]
     shapes = [a.shape for a in (q_weight, k_weight, q_moment, k_moment)]
     parts = pl.pallas_call(
         functools.partial(kernel, n_dp, n_mp, heads),
@@ -439,8 +473,8 @@
             vmem(folded, F32),
             vmem(folded, F32),
             vmem((2 * n_group - 1,) + folded, F32),
-            dma((n_outer, CHUNKS)), dma((n_outer, CHUNKS)),
-            dma((n_outer, CHUNKS)), dma((n_outer, CHUNKS)),
+            dma((n_outer, chunks)), dma((n_outer, chunks)),
+            dma((n_outer, chunks)), dma((n_outer, chunks)),
             dma((2,)), dma((2,)),
             dma((n_dp - 1,)), dma((n_dp - 1,)),
             dma((n_mp - 1,)), dma((n_mp - 1,)),

time: 30.2 us -> 29.4 us (0.974)
  the two profiles are of different devices: /device:TPU:9 before, /device:TPU:0 now
where the time goes in v2:
time: 29.4 us; the launch traced here: 29.3 us
  Pallas kernels  28.6 us (97%)
  between operations  0.64 us (2%)
    pallas_call x1, Pallas kernels, local(): pl.pallas_call(functools.partial(kernel, n_dp, n_mp, heads), out_shape=[v...  27.7 us
    pallas_call x1, Pallas kernels, local(): pl.pallas_call(functools.partial(finish, n_mp), out_shape=[jax.ShapeDtype...  0.89 us

profile of v2, /device:TPU:0, one launch (start us, length us, event | category | flops | bytes accessed | tf_op | source)
XLA Modules:
  0.0 29.3 jit_solution(1142035195353982629)
XLA Ops:
  0.6 27.7 %shard_map.147 = (f32[1,192,128]{2,1,0:T(8,128)S(1)}, f32[1,64,128]{2,1,0:T(8,128)S(1)}, f32[1,192,128]{2,1,0:T(8,128)S(1)}, f32[1,64,128]{2,1,0:T(8,128)S(1)}, ...) custom-call(bf16[2,192,256]{2,1,0:T(8,128)(2,1)} %bitcast.4, bf16[2,64,256]{2,1,0:T(8,128)(2,1)} %bitcast.5, ...), custom_call_target="tpu_custom_call" | custom-call | tf_op jit(solution)/shard_map/pallas_call | solution.py:456
  28.4 0.9 %shard_map.148 = (f32[1,192,128]{2,1,0:T(8,128)}, f32[1,64,128]{2,1,0:T(8,128)}, f32[1,192,128]{2,1,0:T(8,128)}, f32[1,64,128]{2,1,0:T(8,128)}) custom-call(f32[1,192,128]{2,1,0:T(8,128)S(1)} %get-tuple-element.10.qw_ref, f32[1,64,128]{2,1,0:T(8,128)S(1)} %get-tuple-element.11.kw_ref, f32[1,192,128]{2,1,0:T(8,128)S(1)} %get-tuple-element.12.qm_ref, ...), custom_call_target="tpu_custom_call" | custom-call | tf_op jit(solution)/shard_map/pallas_call | solution.py:489

commit v3 on v2

v3 whole, which is shorter than its diff:
```python
import functools
import math

import jax
import jax.numpy as jnp
from jax import lax
from jax.experimental import pallas as pl
from jax.experimental.pallas import tpu as pltpu
from jax.sharding import PartitionSpec as P

ITERS = 5
MOMENTUM = 0.95
STEP_SIZE = 1.0
DECAY = 0.1
CLIP_LEVEL = 0.1
SCORE_SCALE = 1.0 / math.sqrt(192.0)
COEFF_A = 3.4445
COEFF_B = -4.775
COEFF_C = 2.0315
LOWEST = -1e30
MESH = pl.DeviceIdType.MESH
F32 = jnp.float32
BF16 = jnp.bfloat16


def split(value):
    high = value.astype(BF16)
    return high, (value - high.astype(F32)).astype(BF16)


def mm(a, b):
    return jnp.dot(a, b, preferred_element_type=F32)


def mm3(a, b):
    both = mm(a[0], jnp.concatenate([b[0], b[1]], axis=1))
    width = b[0].shape[1]
    return both[:, :width] + (both[:, width:] + mm(a[1], b[0]))


def mm_deep(a, b):
    return mm(
        jnp.concatenate([a[0], a[1], a[0]], axis=1), jnp.concatenate([b[0], b[0], b[1]], axis=0)
    )


def gram_pair(rows):
    high, low = split(rows)
    return mm(high.T, jnp.concatenate([high, low], axis=1))


def gram_of(pair):
    width = pair.shape[0]
    cross = pair[:, width:]
    return pair[:, :width] + (cross + cross.T)


def fold(matrix):
    width = matrix.shape[0]
    half = width // 2
    row = lax.broadcasted_iota(jnp.int32, (half, width), 0)
    lane = lax.broadcasted_iota(jnp.int32, (half, width), 1)
    lower = matrix[half:]
    body = jnp.where(lane >= row, matrix[:half], pltpu.roll(lower, half, 1))
    ends = jnp.sum(jnp.where(lane == row + half, lower, 0.0), axis=0, keepdims=True)
    return jnp.concatenate([body, ends], axis=0)


def unfold(message):
    width = message.shape[1]
    half = width // 2
    row = lax.broadcasted_iota(jnp.int32, (half, width), 0)
    lane = lax.broadcasted_iota(jnp.int32, (half, width), 1)
    body = message[:half]
    ends = jnp.broadcast_to(message[half : half + 1], (half, width))
    top = jnp.where(lane >= row, body, 0.0)
    strict = jnp.where((lane >= half) & (lane - half < row), pltpu.roll(body, half, 1), 0.0)
    one_side = jnp.concatenate([top, jnp.where(lane == row + half, ends, strict)], axis=0)
    full_row = lax.broadcasted_iota(jnp.int32, (width, width), 0)
    full_lane = lax.broadcasted_iota(jnp.int32, (width, width), 1)
    return one_side + jnp.where(full_row == full_lane, 0.0, one_side.T)


def column(row):
    count = row.shape[1]
    spread = jnp.broadcast_to(row, (count, count))
    same = lax.broadcasted_iota(jnp.int32, (count, count), 0) == lax.broadcasted_iota(
        jnp.int32, (count, count), 1
    )
    picked = jnp.where(same, spread, 0).astype(F32)
    return jnp.sum(picked, axis=1, keepdims=True).astype(jnp.int32)


def partner(index, count, step):
    if count & (count - 1):
        return lax.rem(index + step, count)
    result = 0
    bit = 1
    while bit < count:
        held = lax.rem(lax.div(index, bit), 2)
        result = result + bit * ((1 - held) if step & bit else held)
        bit *= 2
    return result


def kernel(
    n_dp, n_mp, heads,
    ql_in, kl_in, qg_in, kg_in, qh_in, kh_in, qp_in, kp_in, qw_in, kw_in, qm_in, km_in,
    qw_out, kw_out, qm_out, km_out, qy_out, ky_out, final, shrink_out,
    latents, grads, act, picks, state, in_sems,
    near_send, near_recv, own, far_recv, raw_recv, peak_send, peak_recv, peak2_send, peak2_recv,
    grams, gram_recv, row_send, row_recv, mix,
    ns_s, ns_r, fs_s, fs_r, rw_r, pk_s, pk_r, pm_s, pm_r, g_s, g_r, y_s, y_r, m_s, m_r,
):
    dp = lax.axis_index("dp")
    mp = lax.axis_index("mp")
    n_outer = n_dp // 2
    outer = lax.div(dp, 2)
    inner = lax.rem(dp, 2)
    core = lax.rem(mp, 2)
    group = lax.div(mp, 2)
    n_group = n_mp // 2
    q_rows = qm_in.shape[1]
    k_rows = km_in.shape[1]
    width = qm_in.shape[2]
    tokens = qg_in.shape[0]
    tall = q_rows + k_rows
    top_rows = pl.ds(0, k_rows)
    low_rows = pl.ds(k_rows, q_rows)
    other_core = mp + 1 - 2 * core

    loads = (
        ((kl_in, latents.at[:, top_rows]), (ql_in, latents.at[:, low_rows])),
        ((kg_in, grads.at[1]), (qg_in, grads.at[0])),
        ((qp_in, picks.at[0]), (kp_in, picks.at[1])),
        ((qh_in, act.at[0]), (kh_in, act.at[1])),
        (
            (km_in.at[0], state.at[1, top_rows]), (qm_in.at[0], state.at[1, low_rows]),
            (kw_in.at[0], state.at[0, top_rows]), (qw_in.at[0], state.at[0, low_rows]),
        ),
    )
    for i, group_of in enumerate(loads):
        for src, dst in group_of:
            pltpu.make_async_copy(src, dst, in_sems.at[i]).start()

    def loaded(*which):
        for i in which:
            ref = (latents, grads, picks, act, state)[i]
            pltpu.make_async_copy(ref, ref, in_sems.at[i]).wait()

    barrier = pltpu.get_barrier_semaphore()
    for step in range(1, n_dp):
        pl.semaphore_signal(
            barrier, inc=1, device_id=(lax.rem(dp + step, n_dp), mp), device_id_type=MESH
        )
    def owner(step):
        across = lax.rem(dp + (step // n_group) * heads, n_dp)
        return across, 2 * lax.rem(group + step, n_group) + core

    for step in range(n_group + 1, 2 * n_group):
        pl.semaphore_signal(barrier, inc=1, device_id=owner(step), device_id_type=MESH)
    for step in range(1, n_mp):
        pl.semaphore_signal(
            barrier, inc=1, device_id=(dp, lax.rem(mp + step, n_mp)), device_id_type=MESH
        )

    def copy(src, dst, send, recv, where):
        return pltpu.make_async_remote_copy(
            src_ref=src, dst_ref=dst, send_sem=send, recv_sem=recv,
            device_id=where, device_id_type=MESH,
        )

    all_peaks = copy(peak_recv, peak_recv, pk_s, pk_r, (dp, other_core))
    all_peaks2 = copy(peak2_recv, peak2_recv, pm_s, pm_r, (dp, other_core))
    all_rows = copy(row_recv, row_recv, y_s, y_r, (dp, other_core))

    def term(dst, spot, to_outer, to_inner):
        slot = 2 * to_outer + to_inner
        half = lax.div(slot, heads)
        cols = pl.ds(pl.multiple_of(lax.rem(slot, heads) * width, width), width)
        first = spot * chunks
        dst[first] = mm(latents[half, :k_rows], grads[1, :, cols])
        rest = mm(latents[half, k_rows:], grads[0, :, cols])
        dst[first + 1 : first + chunks] = rest.reshape(chunks - 1, step_rows, width)

    step_rows = k_rows
    chunks = tall // step_rows
    loaded(0, 1)
    entered = n_dp + n_mp + n_group - 3
    neighbour = (dp + 1 - 2 * inner, mp)
    last = n_outer - 1
    line = n_outer == 4
    inside = lax.rem(lax.div(outer, 2) + lax.rem(outer, 2), 2)
    by = [partner(outer, n_outer, step) for step in range(n_outer)]

    def at(spot, chunk):
        return spot * chunks + chunk

    if line:
        split_to = by[2] + inside * (by[1] - by[2])
        whole_to = by[1] + inside * (by[2] - by[1])
        order = [by[3], split_to, whole_to, by[0]]
        kept = chunks // 2
        spans = [range(chunks), range(kept), range(chunks), range(chunks)]
    else:
        order = by[::-1]
        spans = [range(chunks)] * n_outer

    def near_copy(spot, chunk):
        where = at(spot, chunk)
        return copy(near_send.at[where], near_recv.at[where], ns_s, ns_r.at[where], neighbour)

    def far_copy(spot, slot, chunk, target):
        where = at(slot, chunk)
        return copy(
            own.at[at(spot, chunk)], far_recv.at[where], fs_s, fs_r.at[where],
            (2 * target + inner, mp),
        )

    def raw_copy(which):
        source = (near_send, own)[which]
        return copy(
            source.at[pl.ds(at(1, kept), chunks - kept)], raw_recv.at[which],
            fs_s, rw_r.at[which], (2 * split_to + inner, mp),
        )

    def send_near(spot, which):
        for chunk in which:
            near_copy(spot, chunk).start()

    raw = [raw_copy(0), raw_copy(1)] if line else []
    term(near_send, 0, order[0], 1 - inner)
    pl.semaphore_wait(barrier, entered)
    send_near(0, spans[0])
    if line:
        term(near_send, 1, order[1], 1 - inner)
        raw[0].start()
        term(own, 1, order[1], inner)
        raw[1].start()
        term(near_send, 2, order[2], 1 - inner)

        @pl.when(inside == 1)
        def _():
            send_near(2, spans[2])
            send_near(1, spans[1])

        @pl.when(inside == 0)
        def _():
            send_near(1, spans[1])
            send_near(2, spans[2])

    loaded(2, 3)
    local_heads = picks.shape[1]
    lane = lax.broadcasted_iota(jnp.int32, (1, width), 1)
    peaks = jnp.full((1, width), LOWEST, F32)
    ids = lax.broadcasted_iota(jnp.int32, (picks.shape[3], tokens), 1)
    for head in range(local_heads):
        span = slice(head * width, (head + 1) * width)
        pick_q = (ids == column(picks[0, head])).astype(F32).astype(BF16)
        pick_k = (ids == column(picks[1, head])).astype(F32).astype(BF16)
        score = jnp.sum(
            mm(pick_q, act[0, :, span]) * mm(pick_k, act[1, :, span]), axis=1, keepdims=True
        )
        top = jnp.max(score * SCORE_SCALE, axis=0, keepdims=True)
        peaks = jnp.where(lane == mp * local_heads + head, top, peaks)
    peak_send[...] = peaks
    for step in range(1, n_dp):
        each = copy(
            peak_send, peak_recv.at[step - 1], pk_s, pk_r,
            (lax.rem(dp + step, n_dp), mp),
        )
        each.start()

    if line:
        term(near_send, last, order[last], 1 - inner)
        send_near(last, range(kept))
    else:
        for spot in range(1, n_outer):
            term(near_send, spot, order[spot], 1 - inner)
            send_near(spot, spans[spot])
    for spot in range(n_outer):
        if not (line and spot == 1):
            term(own, spot, order[spot], inner)

    def meet(spot, chunk):
        near_copy(spot, chunk).wait_recv()
        where = at(spot, chunk)
        own[where] = own[where] + near_recv[where]

    def gather(slot, chunk):
        far_copy(0, slot, chunk, outer).wait_recv()
        return far_recv[at(slot, chunk)]

    relay = 3

    def pass_on(spot):
        for chunk in spans[spot]:
            meet(spot, chunk)
            far_copy(spot, spot, chunk, order[spot]).start()

    if line:
        first_to = by[1] + inside * (by[3] - by[1])
        for chunk in spans[0]:
            meet(0, chunk)
            far_copy(0, relay * (1 - inside), chunk, first_to).start()
        raw[0].wait_recv()
        low = pl.ds(at(last, kept), chunks - kept)
        near_send[low] = near_send[low] + raw_recv[0]
        send_near(last, range(kept, chunks))

        @pl.when(inside == 1)
        def _():
            for chunk in spans[2]:
                own[at(2, chunk)] = own[at(2, chunk)] + gather(relay, chunk)
                meet(2, chunk)
                far_copy(2, 2, chunk, whole_to).start()
            pass_on(1)
            for chunk in spans[0]:
                own[at(last, chunk)] = own[at(last, chunk)] + gather(0, chunk)

        @pl.when(inside == 0)
        def _():
            pass_on(1)
            pass_on(2)

        raw[1].wait_recv()
        own[low] = own[low] + raw_recv[1]
    else:
        for spot in range(last):
            pass_on(spot)

    loaded(4)

    def complete(chunk):
        where = at(last, chunk)
        meet(last, chunk)
        if line:
            if chunk in spans[1]:
                own[where] = own[where] + gather(1, chunk)
            total = own[where] + gather(2, chunk)
        else:
            total = own[where]
            for spot in range(last):
                total = total + gather(spot, chunk)
        rows = MOMENTUM * state[1, chunk * step_rows : (chunk + 1) * step_rows] + total
        if not chunk:
            km_out[0] = rows
        else:
            qm_out[0, (chunk - 1) * step_rows : chunk * step_rows] = rows
        return gram_pair(rows)

    swap = copy(grams.at[1 - core], gram_recv, g_s, g_r, (dp, other_core))
    grams[1] = fold(gram_of(complete(0)))

    @pl.when(core == 0)
    def _():
        swap.start()

    pair = complete(1)
    for chunk in range(2, chunks):
        pair = pair + complete(chunk)
    grams[0] = fold(gram_of(pair))

    @pl.when(core == 1)
    def _():
        swap.start()

    swap.wait_recv()
    whole = grams[core] + gram_recv[...]
    row_send[...] = whole
    for step in range(1, 2 * n_group):
        each = copy(
            row_send, row_recv.at[step - 1], y_s, y_r, owner(step)
        )
        each.start()
    all_peaks.wait_recv()
    peaks = jnp.maximum(peaks, jnp.max(peak_recv[...], axis=0))
    peak2_send[...] = peaks
    for step in range(1, n_mp):
        each = copy(
            peak2_send, peak2_recv.at[step - 1], pm_s, pm_r,
            (dp, lax.rem(mp + step, n_mp)),
        )
        each.start()

    all_rows.wait_recv()
    whole = unfold(whole + jnp.sum(row_recv[...], axis=0))

    eye = (
        lax.broadcasted_iota(jnp.int32, (width, width), 0)
        == lax.broadcasted_iota(jnp.int32, (width, width), 1)
    ).astype(F32)
    trace = jnp.sum(jnp.sum(whole * eye, axis=0, keepdims=True), axis=1, keepdims=True)
    scale = 1.0 / jnp.sqrt(trace + 1.0)
    current = whole * (scale * scale)
    mixed = None
    swap2 = [
        copy(ref.at[core], ref.at[core], m_s, m_r.at[i], (dp, other_core))
        for i, ref in enumerate((mix, final))
    ]
    for step in range(ITERS):
        parts = split(current)
        square = mm_deep(parts, parts)
        poly = COEFF_A * eye + COEFF_B * current + COEFF_C * square
        if step + 1 == ITERS:
            break
        pair = split(poly)
        mixed = poly * scale if mixed is None else mm_deep(split(mixed), pair)
        if step + 2 == ITERS:
            mix[core] = mixed
            swap2[0].start()
        current = mm_deep(split(mm_deep(pair, parts)), pair)
    final[core] = poly
    swap2[1].start()
    all_peaks2.wait_recv()
    peaks = jnp.maximum(peaks, jnp.max(peak2_recv[...], axis=0))
    mine = jnp.where(lane == lax.rem(dp, heads), peaks, LOWEST)
    peak = jnp.max(jnp.max(mine, axis=0, keepdims=True), axis=1, keepdims=True)
    shrink = jnp.sqrt(CLIP_LEVEL / jnp.maximum(peak, CLIP_LEVEL))
    keep = 1.0 - STEP_SIZE * DECAY
    shrink_out[...] = jnp.broadcast_to(shrink, shrink_out.shape)
    qw_out[0] = (state[0, k_rows:] * keep) * shrink
    kw_out[0] = (state[0, :k_rows] * keep) * shrink
    swap2[0].wait_recv()
    for which, (moment, part_out) in enumerate(((qm_out, qy_out), (km_out, ky_out))):
        part_out[0] = mm3(split(moment[0]), split(mix[which]))
    swap2[1].wait_recv()
    sent = sum(len(span) for span in spans)
    passed = sent - len(spans[last]) + (2 * (chunks - kept) if line else 0)
    for count, ref, sem in ((sent, near_send, ns_s), (passed, own, fs_s)):
        part = ref.at[pl.ds(0, count)]
        copy(part, part, sem, sem, (dp, other_core)).wait_send()
    copy(mix, mix, m_s, m_s, (dp, other_core)).wait_send()
    for each in (all_peaks, all_peaks2, swap, all_rows):
        each.wait_send()


def finish(
    n_mp, qw_ref, kw_ref, qm_ref, km_ref, qy_ref, ky_ref, final_ref, shrink_ref,
    qw_out, kw_out, qm_out, km_out, qw_new, kw_new, sems,
):
    stores = [
        pltpu.make_async_copy(src, dst, sems.at[i])
        for i, (src, dst) in enumerate((
            (qm_ref, qm_out), (km_ref, km_out), (kw_new, kw_out), (qw_new, qw_out),
        ))
    ]
    stores[0].start()
    stores[1].start()
    groups = ((1, kw_ref, ky_ref, kw_new, stores[2]), (0, qw_ref, qy_ref, qw_new, stores[3]))
    for which, weight, part, weight_new, store in groups:
        size = STEP_SIZE * 0.2 * math.sqrt(2 * n_mp * part.shape[1])
        ortho = mm3(split(part[0]), split(final_ref[which]))
        weight_new[0] = weight[0] - (size * ortho) * shrink_ref[...]
        store.start()
    for each in stores:
        each.wait()


def local(
    q_latent, kv_latent, q_head_grad, k_head_grad, q_heads, k_heads,
    query_pick, key_pick, q_weight, k_weight, q_moment, k_moment,
):
    n_dp = lax.axis_size("dp")
    n_mp = lax.axis_size("mp")
    heads = n_dp // 2
    n_outer = n_dp // 2
    n_group = n_mp // 2
    rows = q_latent.shape[2] + kv_latent.shape[2]
    width = q_moment.shape[2]
    operands = (
        q_latent.transpose(1, 2, 0), kv_latent.transpose(1, 2, 0), q_head_grad, k_head_grad,
        q_heads, k_heads, query_pick.transpose(2, 0, 1), key_pick.transpose(2, 0, 1),
        q_weight, k_weight, q_moment, k_moment,
    )
    vmem = pltpu.VMEM
    dma = pltpu.SemaphoreType.DMA
    square = (width, width)
    folded = (width // 2 + 1, width)
    tile = (1, width)
    tokens = q_latent.shape[0]
    k_rows = k_moment.shape[1]
    chunks = rows // k_rows

    def blocks(count):
        return vmem((count, k_rows, width), F32)

    shapes = [a.shape for a in (q_weight, k_weight, q_moment, k_moment)]
    parts = pl.pallas_call(
        functools.partial(kernel, n_dp, n_mp, heads),
        out_shape=[vmem(shape, F32) for shape in shapes + shapes[2:] + [(2,) + square, tile]],
        in_specs=[pl.BlockSpec(memory_space=pl.ANY)] * 12,
        out_specs=[pl.BlockSpec(memory_space=vmem)] * 8,
        scratch_shapes=[
            vmem((2, rows, tokens), BF16),
            vmem((2,) + q_head_grad.shape, BF16),
            vmem((2,) + q_heads.shape, BF16),
            vmem((2,) + operands[6].shape, jnp.int32),
            vmem((2, rows, width), F32),
            dma((5,)),
            blocks(n_outer * chunks), blocks(n_outer * chunks),
            blocks(n_outer * chunks), blocks(n_outer * chunks),
            vmem((2, chunks - chunks // 2, k_rows, width), F32),
            vmem(tile, F32),
            vmem((n_dp - 1,) + tile, F32),
            vmem(tile, F32),
            vmem((n_mp - 1,) + tile, F32),
            vmem((2,) + folded, F32),
            vmem(folded, F32),
            vmem(folded, F32),
            vmem((2 * n_group - 1,) + folded, F32),
            vmem((2,) + square, F32),
            dma, dma((n_outer * chunks,)),
            dma, dma((n_outer * chunks,)),
            dma((2,)),
            dma, dma, dma, dma, dma, dma, dma, dma,
            dma, dma((2,)),
        ],
        compiler_params=pltpu.CompilerParams(
            collective_id=0, has_side_effects=True, vmem_limit_bytes=56 * 1024 * 1024
        ),
    )(*operands)
    return pl.pallas_call(
        functools.partial(finish, n_mp),
        out_shape=[jax.ShapeDtypeStruct(shape, F32) for shape in shapes],
        in_specs=[pl.BlockSpec(memory_space=vmem)] * 8,
        out_specs=[pl.BlockSpec(memory_space=pl.ANY)] * 4,
        scratch_shapes=[vmem(shape, F32) for shape in shapes[:2]] + [dma((4,))],
    )(*[pltpu.with_memory_space_constraint(part, vmem) for part in parts])


def solution(mesh):
    rows3 = P("dp", "mp", None)
    in_specs = (
        P("dp", None, "mp"), P("dp", None, "mp"), P("dp", None), P("dp", None),
        P("dp", "mp"), P("dp", "mp"), P("dp", None, "mp"), P("dp", None, "mp"),
        rows3, rows3, rows3, rows3,
    )
    return jax.shard_map(
        lambda *args: tuple(local(*args)),
        mesh=mesh, in_specs=in_specs, out_specs=(rows3,) * 4, check_vma=False,
    )
```

time: 29.4 us -> 28.7 us (0.976)
  Pallas kernels: 28.6 us -> 27.9 us
    pallas_call x1, Pallas kernels: 27.7 us -> 27 us  [local(): pl.pallas_call(functools.partial(kernel, n_dp, n_mp, heads), out_shape=[v...]
where the time goes in v3:
time: 28.7 us; the launch traced here: 28.6 us
  Pallas kernels  27.9 us (97%)
  between operations  0.64 us (2%)
    pallas_call x1, Pallas kernels, local(): pl.pallas_call(functools.partial(kernel, n_dp, n_mp, heads), out_shape=[v...  27 us
    pallas_call x1, Pallas kernels, local(): pl.pallas_call(functools.partial(finish, n_mp), out_shape=[jax.ShapeDtype...  0.89 us

profile of v3, /device:TPU:0, one launch (start us, length us, event | category | flops | bytes accessed | tf_op | source)
XLA Modules:
  0.0 28.6 jit_solution(128768412520677983)
XLA Ops:
  0.6 27.0 %shard_map.147 = (f32[1,192,128]{2,1,0:T(8,128)S(1)}, f32[1,64,128]{2,1,0:T(8,128)S(1)}, f32[1,192,128]{2,1,0:T(8,128)S(1)}, f32[1,64,128]{2,1,0:T(8,128)S(1)}, ...) custom-call(bf16[2,192,256]{2,1,0:T(8,128)(2,1)} %bitcast.4, ...), custom_call_target="tpu_custom_call" | custom-call | tf_op jit(solution)/shard_map/pallas_call | solution.py:489
  27.7 0.9 %shard_map.148 = (f32[1,192,128]{2,1,0:T(8,128)}, f32[1,64,128]{2,1,0:T(8,128)}, f32[1,192,128]{2,1,0:T(8,128)}, f32[1,64,128]{2,1,0:T(8,128)}) custom-call(f32[1,192,128]{2,1,0:T(8,128)S(1)} %get-tuple-element.12.qw_ref, f32[1,64,128]{2,1,0:T(8,128)S(1)} %get-tuple-element.13.kw_ref, f32[1,192,128]{2,1,0:T(8,128)S(1)} %get-tuple-element.14.qm_ref, ...), custom_call_target="tpu_custom_call" | custom-call | tf_op jit(solution)/shard_map/pallas_call | solution.py:523

commit v4 on v3

--- a/solution.py
+++ b/solution.py
@@ -81,7 +81,7 @@
     return one_side + jnp.where(full_row == full_lane, 0.0, one_side.T)
 
 
-def column(row):
+def spread_down(row):
     count = row.shape[1]
     spread = jnp.broadcast_to(row, (count, count))
     same = lax.broadcasted_iota(jnp.int32, (count, count), 0) == lax.broadcasted_iota(
@@ -108,9 +108,9 @@
     ql_in, kl_in, qg_in, kg_in, qh_in, kh_in, qp_in, kp_in, qw_in, kw_in, qm_in, km_in,
     qw_out, kw_out, qm_out, km_out, qy_out, ky_out, final, shrink_out,
     latents, grads, act, picks, state, in_sems,
-    near_send, near_recv, own, far_recv, raw_recv, peak_send, peak_recv, peak2_send, peak2_recv,
-    grams, gram_recv, row_send, row_recv, mix,
-    ns_s, ns_r, fs_s, fs_r, rw_r, pk_s, pk_r, pm_s, pm_r, g_s, g_r, y_s, y_r, m_s, m_r,
+    near_send, near_recv, own, relay_recv, raw_recv, fin, base, back_send, back_recv, peak_send, peak_recv, peak2_send, peak2_recv,
+    row_send, row_recv, mix,
+    ns_s, ns_r, fs_s, fin_r, rl_r, rw_r, b_s, b_r, bk_s, bk_r, pk_s, pk_r, pm_s, pm_r, y_s, y_r, m_s, m_r,
 ):
     dp = lax.axis_index("dp")
     mp = lax.axis_index("mp")
@@ -150,9 +150,10 @@
 
     barrier = pltpu.get_barrier_semaphore()
     for step in range(1, n_dp):
-        pl.semaphore_signal(
-            barrier, inc=1, device_id=(lax.rem(dp + step, n_dp), mp), device_id_type=MESH
-        )
+        for column in (mp, other_core):
+            pl.semaphore_signal(
+                barrier, inc=1, device_id=(lax.rem(dp + step, n_dp), column), device_id_type=MESH
+            )
     def owner(step):
         across = lax.rem(dp + (step // n_group) * heads, n_dp)
         return across, 2 * lax.rem(group + step, n_group) + core
@@ -186,8 +187,10 @@
     step_rows = k_rows
     chunks = tall // step_rows
     loaded(0, 1)
-    entered = n_dp + n_mp + n_group - 3
-    neighbour = (dp + 1 - 2 * inner, mp)
+    entered = 2 * (n_dp - 1) + (n_mp - 1) + (n_group - 1)
+    across_x = dp + 1 - 2 * inner
+    neighbour = (across_x, mp)
+    partner_core = (dp, other_core)
     last = n_outer - 1
     line = n_outer == 4
     inside = lax.rem(lax.div(outer, 2) + lax.rem(outer, 2), 2)
@@ -210,33 +213,47 @@
         where = at(spot, chunk)
         return copy(near_send.at[where], near_recv.at[where], ns_s, ns_r.at[where], neighbour)
 
-    def far_copy(spot, slot, chunk, target):
-        where = at(slot, chunk)
+    def home(chunk):
+        return 2 * group + (1 if chunk else 0)
+
+    def final_copy(source, spot, slot, chunk, sent, to):
         return copy(
-            own.at[at(spot, chunk)], far_recv.at[where], fs_s, fs_r.at[where],
-            (2 * target + inner, mp),
-        )
-
-    def raw_copy(which):
-        source = (near_send, own)[which]
+            source.at[at(spot, chunk)], fin.at[slot, chunk, core], sent, fin_r.at[slot, chunk],
+            (to, home(chunk)),
+        )
+
+    def far_copy(spot, chunk, target):
+        return final_copy(own, spot, spot, chunk, fs_s, 2 * target + inner)
+
+    def send_last(which):
+        for chunk in which:
+            final_copy(near_send, last, last, chunk, ns_s, across_x).start()
+
+    def relay_copy(chunk):
         return copy(
-            source.at[pl.ds(at(1, kept), chunks - kept)], raw_recv.at[which],
-            fs_s, rw_r.at[which], (2 * split_to + inner, mp),
+            own.at[at(0, chunk)], relay_recv.at[chunk], fs_s, rl_r.at[chunk],
+            (2 * by[1] + inner, mp),
+        )
+
+    def raw_copy():
+        return copy(
+            near_send.at[pl.ds(at(1, kept), chunks - kept)], raw_recv, fs_s, rw_r,
+            (2 * split_to + inner, mp),
         )
 
     def send_near(spot, which):
         for chunk in which:
             near_copy(spot, chunk).start()
 
-    raw = [raw_copy(0), raw_copy(1)] if line else []
     term(near_send, 0, order[0], 1 - inner)
     pl.semaphore_wait(barrier, entered)
     send_near(0, spans[0])
     if line:
         term(near_send, 1, order[1], 1 - inner)
-        raw[0].start()
+        raw_copy().start()
         term(own, 1, order[1], inner)
-        raw[1].start()
+        for chunk in range(kept, chunks):
+            far_copy(1, chunk, split_to).start()
         term(near_send, 2, order[2], 1 - inner)
 
         @pl.when(inside == 1)
@@ -256,8 +273,8 @@
     ids = lax.broadcasted_iota(jnp.int32, (picks.shape[3], tokens), 1)
     for head in range(local_heads):
         span = slice(head * width, (head + 1) * width)
-        pick_q = (ids == column(picks[0, head])).astype(F32).astype(BF16)
-        pick_k = (ids == column(picks[1, head])).astype(F32).astype(BF16)
+        pick_q = (ids == spread_down(picks[0, head])).astype(F32).astype(BF16)
+        pick_k = (ids == spread_down(picks[1, head])).astype(F32).astype(BF16)
         score = jnp.sum(
             mm(pick_q, act[0, :, span]) * mm(pick_k, act[1, :, span]), axis=1, keepdims=True
         )
@@ -273,106 +290,138 @@
 
     if line:
         term(near_send, last, order[last], 1 - inner)
-        send_near(last, range(kept))
+        send_last(range(kept))
     else:
         for spot in range(1, n_outer):
             term(near_send, spot, order[spot], 1 - inner)
-            send_near(spot, spans[spot])
+            if spot < last:
+                send_near(spot, spans[spot])
+        send_last(range(chunks))
     for spot in range(n_outer):
         if not (line and spot == 1):
             term(own, spot, order[spot], inner)
+
+    loaded(4)
+    for chunk in range(chunks):
+        moment = state[1, chunk * step_rows : (chunk + 1) * step_rows]
+        own[at(last, chunk)] = MOMENTUM * moment + own[at(last, chunk)]
+
+    def on_core(which):
+        return pl.when(core == which)
+
+    def shares(which):
+        return pl.ds(0, 1) if which else pl.ds(1, chunks - 1)
+
+    def base_copy(which):
+        rows = shares(which)
+        source = own.at[pl.ds(at(last, rows.start), rows.size)]
+        return copy(source, base.at[rows], b_s, b_r, partner_core)
+
+    def back_copy(which):
+        rows = pl.ds(0, shares(1 - which).size)
+        return copy(back_send.at[rows], back_recv.at[rows], bk_s, bk_r, partner_core)
+
+    for which in range(2):
+
+        @on_core(which)
+        def _():
+            base_copy(which).start()
 
     def meet(spot, chunk):
         near_copy(spot, chunk).wait_recv()
         where = at(spot, chunk)
         own[where] = own[where] + near_recv[where]
 
-    def gather(slot, chunk):
-        far_copy(0, slot, chunk, outer).wait_recv()
-        return far_recv[at(slot, chunk)]
-
-    relay = 3
+    def arrived(slot, chunk):
+        ref = fin.at[slot, chunk]
+        copy(ref, ref, fs_s, fin_r.at[slot, chunk], partner_core).wait_recv()
+        return fin[slot, chunk]
 
     def pass_on(spot):
         for chunk in spans[spot]:
             meet(spot, chunk)
-            far_copy(spot, spot, chunk, order[spot]).start()
+            far_copy(spot, chunk, order[spot]).start()
 
     if line:
-        first_to = by[1] + inside * (by[3] - by[1])
         for chunk in spans[0]:
             meet(0, chunk)
-            far_copy(0, relay * (1 - inside), chunk, first_to).start()
-        raw[0].wait_recv()
+
+            @pl.when(inside == 1)
+            def _():
+                far_copy(0, chunk, by[3]).start()
+
+            @pl.when(inside == 0)
+            def _():
+                relay_copy(chunk).start()
+
+        raw_copy().wait_recv()
         low = pl.ds(at(last, kept), chunks - kept)
-        near_send[low] = near_send[low] + raw_recv[0]
-        send_near(last, range(kept, chunks))
+        near_send[low] = near_send[low] + raw_recv[...]
+        send_last(range(kept, chunks))
 
         @pl.when(inside == 1)
         def _():
             for chunk in spans[2]:
-                own[at(2, chunk)] = own[at(2, chunk)] + gather(relay, chunk)
+                relay_copy(chunk).wait_recv()
+                own[at(2, chunk)] = own[at(2, chunk)] + relay_recv[chunk]
                 meet(2, chunk)
-                far_copy(2, 2, chunk, whole_to).start()
+                far_copy(2, chunk, whole_to).start()
             pass_on(1)
-            for chunk in spans[0]:
-                own[at(last, chunk)] = own[at(last, chunk)] + gather(0, chunk)
 
         @pl.when(inside == 0)
         def _():
             pass_on(1)
             pass_on(2)
 
-        raw[1].wait_recv()
-        own[low] = own[low] + raw_recv[1]
     else:
         for spot in range(last):
             pass_on(spot)
 
-    loaded(4)
-
-    def complete(chunk):
-        where = at(last, chunk)
-        meet(last, chunk)
-        if line:
-            if chunk in spans[1]:
-                own[where] = own[where] + gather(1, chunk)
-            total = own[where] + gather(2, chunk)
+    def complete(which, chunk):
+        added = [arrived(slot, chunk) for slot in ((1, 2, last) if line else range(n_outer))]
+        mine = own[at(last, chunk)]
+        other = base[chunk]
+        for each in added:
+            mine = mine + each[which]
+            other = other + each[1 - which]
+        if which:
+            qm_out[0, (chunk - 1) * step_rows : chunk * step_rows] = mine
+            back_send[chunk - 1] = other
         else:
-            total = own[where]
-            for spot in range(last):
-                total = total + gather(spot, chunk)
-        rows = MOMENTUM * state[1, chunk * step_rows : (chunk + 1) * step_rows] + total
-        if not chunk:
-            km_out[0] = rows
-        else:
-            qm_out[0, (chunk - 1) * step_rows : chunk * step_rows] = rows
-        return gram_pair(rows)
-
-    swap = copy(grams.at[1 - core], gram_recv, g_s, g_r, (dp, other_core))
-    grams[1] = fold(gram_of(complete(0)))
-
-    @pl.when(core == 0)
-    def _():
-        swap.start()
-
-    pair = complete(1)
-    for chunk in range(2, chunks):
-        pair = pair + complete(chunk)
-    grams[0] = fold(gram_of(pair))
-
-    @pl.when(core == 1)
-    def _():
-        swap.start()
-
-    swap.wait_recv()
-    whole = grams[core] + gram_recv[...]
-    row_send[...] = whole
+            km_out[0] = mine
+            back_send[chunk] = other
+        return gram_pair(jnp.concatenate([mine, other], axis=0))
+
+    for which, members in enumerate((range(1), range(1, chunks))):
+
+        @on_core(which)
+        def _():
+            base_copy(1 - which).wait_recv()
+            if line:
+
+                @pl.when(inside == 1)
+                def _():
+                    for chunk in members:
+                        early = arrived(0, chunk)
+                        own[at(last, chunk)] = own[at(last, chunk)] + early[which]
+                        base[chunk] = base[chunk] + early[1 - which]
+
+            pair = complete(which, members[0])
+            for chunk in members[1:]:
+                pair = pair + complete(which, chunk)
+            row_send[...] = fold(gram_of(pair))
+
     for step in range(1, 2 * n_group):
         each = copy(
             row_send, row_recv.at[step - 1], y_s, y_r, owner(step)
         )
         each.start()
+    for which in range(2):
+
+        @on_core(which)
+        def _():
+            back_copy(which).start()
+
     all_peaks.wait_recv()
     peaks = jnp.maximum(peaks, jnp.max(peak_recv[...], axis=0))
     peak2_send[...] = peaks
@@ -383,8 +432,18 @@
         )
         each.start()
 
+    @on_core(0)
+    def _():
+        back_copy(1).wait_recv()
+        qm_out[0] = back_recv[...].reshape(q_rows, width)
+
+    @on_core(1)
+    def _():
+        back_copy(0).wait_recv()
+        km_out[0] = back_recv[0]
+
     all_rows.wait_recv()
-    whole = unfold(whole + jnp.sum(row_recv[...], axis=0))
+    whole = unfold(row_send[...] + jnp.sum(row_recv[...], axis=0))
 
     eye = (
         lax.broadcasted_iota(jnp.int32, (width, width), 0)
@@ -395,7 +454,7 @@
     current = whole * (scale * scale)
     mixed = None
     swap2 = [
-        copy(ref.at[core], ref.at[core], m_s, m_r.at[i], (dp, other_core))
+        copy(ref.at[1 - core], ref.at[1 - core], m_s, m_r.at[i], (dp, other_core))
         for i, ref in enumerate((mix, final))
     ]
     for step in range(ITERS):
@@ -407,10 +466,10 @@
         pair = split(poly)
         mixed = poly * scale if mixed is None else mm_deep(split(mixed), pair)
         if step + 2 == ITERS:
-            mix[core] = mixed
+            mix[1 - core] = mixed
             swap2[0].start()
         current = mm_deep(split(mm_deep(pair, parts)), pair)
-    final[core] = poly
+    final[1 - core] = poly
     swap2[1].start()
     all_peaks2.wait_recv()
     peaks = jnp.maximum(peaks, jnp.max(peak2_recv[...], axis=0))
@@ -431,8 +490,14 @@
         part = ref.at[pl.ds(0, count)]
         copy(part, part, sem, sem, (dp, other_core)).wait_send()
     copy(mix, mix, m_s, m_s, (dp, other_core)).wait_send()
-    for each in (all_peaks, all_peaks2, swap, all_rows):
+    for each in (all_peaks, all_peaks2, all_rows):
         each.wait_send()
+    for which in range(2):
+
+        @on_core(which)
+        def _():
+            base_copy(which).wait_send()
+            back_copy(which).wait_send()
 
 
 def finish(
@@ -498,22 +563,20 @@
             vmem((2,) + operands[6].shape, jnp.int32),
             vmem((2, rows, width), F32),
             dma((5,)),
-            blocks(n_outer * chunks), blocks(n_outer * chunks),
-            blocks(n_outer * chunks), blocks(n_outer * chunks),
-            vmem((2, chunks - chunks // 2, k_rows, width), F32),
+            blocks(n_outer * chunks), blocks((n_outer - 1) * chunks), blocks(n_outer * chunks),
+            blocks(chunks), blocks(chunks - chunks // 2),
+            vmem((n_outer, chunks, 2, k_rows, width), F32),
+            blocks(chunks), blocks(chunks - 1), blocks(chunks - 1),
             vmem(tile, F32),
             vmem((n_dp - 1,) + tile, F32),
             vmem(tile, F32),
             vmem((n_mp - 1,) + tile, F32),
-            vmem((2,) + folded, F32),
-            vmem(folded, F32),
             vmem(folded, F32),
             vmem((2 * n_group - 1,) + folded, F32),
             vmem((2,) + square, F32),
-            dma, dma((n_outer * chunks,)),
-            dma, dma((n_outer * chunks,)),
-            dma((2,)),
-            dma, dma, dma, dma, dma, dma, dma, dma,
+            dma, dma(((n_outer - 1) * chunks,)),
+            dma, dma((n_outer, chunks)), dma((chunks,)), dma,
+            dma, dma, dma, dma, dma, dma, dma, dma, dma, dma,
             dma, dma((2,)),
         ],
         compiler_params=pltpu.CompilerParams(

time: 28.7 us -> 28.5 us (level)
  the two profiles are of different devices: /device:TPU:0 before, /device:TPU:9 now
where the time goes in v4:
time: 28.5 us; the launch traced here: 28.4 us
  Pallas kernels  27.7 us (97%)
  between operations  0.64 us (2%)
    pallas_call x1, Pallas kernels, local(): pl.pallas_call(functools.partial(kernel, n_dp, n_mp, heads), out_shape=[v...  26.9 us
    pallas_call x1, Pallas kernels, local(): pl.pallas_call(functools.partial(finish, n_mp), out_shape=[jax.ShapeDtype...  0.89 us

profile of v4, /device:TPU:9, one launch (start us, length us, event | category | flops | bytes accessed | tf_op | source)
XLA Modules:
  0.0 28.4 jit_solution(15880330909873812239)
XLA Ops:
  0.6 26.9 %shard_map.147 = (f32[1,192,128]{2,1,0:T(8,128)S(1)}, f32[1,64,128]{2,1,0:T(8,128)S(1)}, f32[1,192,128]{2,1,0:T(8,128)S(1)}, f32[1,64,128]{2,1,0:T(8,128)S(1)}, ...) custom-call(bf16[2,192,256]{2,1,0:T(8,128)(2,1)} %bitcast.4, ...), custom_call_target="tpu_custom_call" | custom-call | tf_op jit(solution)/shard_map/pallas_call | solution.py:554
  27.5 0.9 %shard_map.148 = (f32[1,192,128]{2,1,0:T(8,128)}, f32[1,64,128]{2,1,0:T(8,128)}, f32[1,192,128]{2,1,0:T(8,128)}, f32[1,64,128]{2,1,0:T(8,128)}) custom-call(f32[1,192,128]{2,1,0:T(8,128)S(1)} %get-tuple-element.12.qw_ref, f32[1,64,128]{2,1,0:T(8,128)S(1)} %get-tuple-element.13.kw_ref, f32[1,192,128]{2,1,0:T(8,128)S(1)} %get-tuple-element.14.qm_ref, ...), custom_call_target="tpu_custom_call" | custom-call | tf_op jit(solution)/shard_map/pallas_call | solution.py:586

commit v5 on v4

--- a/solution.py
+++ b/solution.py
@@ -256,15 +256,8 @@
             far_copy(1, chunk, split_to).start()
         term(near_send, 2, order[2], 1 - inner)
 
-        @pl.when(inside == 1)
-        def _():
-            send_near(2, spans[2])
-            send_near(1, spans[1])
-
-        @pl.when(inside == 0)
-        def _():
-            send_near(1, spans[1])
-            send_near(2, spans[2])
+        send_near(1, spans[1])
+        send_near(2, spans[2])
 
     loaded(2, 3)
     local_heads = picks.shape[1]
@@ -343,35 +336,30 @@
             far_copy(spot, chunk, order[spot]).start()
 
     if line:
-        for chunk in spans[0]:
-            meet(0, chunk)
-
-            @pl.when(inside == 1)
-            def _():
-                far_copy(0, chunk, by[3]).start()
-
-            @pl.when(inside == 0)
-            def _():
-                relay_copy(chunk).start()
-
-        raw_copy().wait_recv()
-        low = pl.ds(at(last, kept), chunks - kept)
-        near_send[low] = near_send[low] + raw_recv[...]
-        send_last(range(kept, chunks))
-
-        @pl.when(inside == 1)
-        def _():
+        def forward(held):
+            for chunk in spans[0]:
+                meet(0, chunk)
+                if held:
+                    far_copy(0, chunk, by[3]).start()
+                else:
+                    relay_copy(chunk).start()
+            pass_on(1)
+            raw_copy().wait_recv()
+            low = pl.ds(at(last, kept), chunks - kept)
+            near_send[low] = near_send[low] + raw_recv[...]
+            send_last(range(kept, chunks))
             for chunk in spans[2]:
-                relay_copy(chunk).wait_recv()
-                own[at(2, chunk)] = own[at(2, chunk)] + relay_recv[chunk]
+                if held:
+                    relay_copy(chunk).wait_recv()
+                    own[at(2, chunk)] = own[at(2, chunk)] + relay_recv[chunk]
                 meet(2, chunk)
                 far_copy(2, chunk, whole_to).start()
-            pass_on(1)
-
-        @pl.when(inside == 0)
-        def _():
-            pass_on(1)
-            pass_on(2)
+
+        for held in range(2):
+
+            @pl.when(inside == held)
+            def _():
+                forward(held)
 
     else:
         for spot in range(last):

time: 28.5 us -> 26.8 us (0.940)
  the two profiles are of different devices: /device:TPU:9 before, /device:TPU:0 now
where the time goes in v5:
time: 26.8 us; the launch traced here: 26.6 us
  Pallas kernels  26 us (97%)
  between operations  0.64 us (2%)
    pallas_call x1, Pallas kernels, local(): pl.pallas_call(functools.partial(kernel, n_dp, n_mp, heads), out_shape=[v...  25.1 us
    pallas_call x1, Pallas kernels, local(): pl.pallas_call(functools.partial(finish, n_mp), out_shape=[jax.ShapeDtype...  0.89 us

profile of v5, /device:TPU:0, one launch (start us, length us, event | category | flops | bytes accessed | tf_op | source)
XLA Modules:
  0.0 26.6 jit_solution(1432644114822490835)
XLA Ops:
  0.6 25.1 %shard_map.147 = (f32[1,192,128]{2,1,0:T(8,128)S(1)}, f32[1,64,128]{2,1,0:T(8,128)S(1)}, f32[1,192,128]{2,1,0:T(8,128)S(1)}, f32[1,64,128]{2,1,0:T(8,128)S(1)}, ...) custom-call(bf16[2,192,256]{2,1,0:T(8,128)(2,1)} %bitcast.4, ...), custom_call_target="tpu_custom_call" | custom-call | tf_op jit(solution)/shard_map/pallas_call | solution.py:542
  25.7 0.9 %shard_map.148 = (f32[1,192,128]{2,1,0:T(8,128)}, f32[1,64,128]{2,1,0:T(8,128)}, f32[1,192,128]{2,1,0:T(8,128)}, f32[1,64,128]{2,1,0:T(8,128)}) custom-call(f32[1,192,128]{2,1,0:T(8,128)S(1)} %get-tuple-element.12.qw_ref, f32[1,64,128]{2,1,0:T(8,128)S(1)} %get-tuple-element.13.kw_ref, f32[1,192,128]{2,1,0:T(8,128)S(1)} %get-tuple-element.14.qm_ref, ...), custom_call_target="tpu_custom_call" | custom-call | tf_op jit(solution)/shard_map/pallas_call | solution.py:574

commit v6 on v5

--- a/solution.py
+++ b/solution.py
@@ -44,15 +44,10 @@
     )
 
 
-def gram_pair(rows):
+def gram(rows):
     high, low = split(rows)
-    return mm(high.T, jnp.concatenate([high, low], axis=1))
-
-
-def gram_of(pair):
-    width = pair.shape[0]
-    cross = pair[:, width:]
-    return pair[:, :width] + (cross + cross.T)
+    left = jnp.concatenate([high, low, high], axis=0)
+    return mm(left.T, jnp.concatenate([high, high, low], axis=0))
 
 
 def fold(matrix):
@@ -175,14 +170,16 @@
     all_peaks2 = copy(peak2_recv, peak2_recv, pm_s, pm_r, (dp, other_core))
     all_rows = copy(row_recv, row_recv, y_s, y_r, (dp, other_core))
 
-    def term(dst, spot, to_outer, to_inner):
+    def term(dst, spot, to_outer, to_inner, parts=(0, 1)):
         slot = 2 * to_outer + to_inner
         half = lax.div(slot, heads)
         cols = pl.ds(pl.multiple_of(lax.rem(slot, heads) * width, width), width)
         first = spot * chunks
-        dst[first] = mm(latents[half, :k_rows], grads[1, :, cols])
-        rest = mm(latents[half, k_rows:], grads[0, :, cols])
-        dst[first + 1 : first + chunks] = rest.reshape(chunks - 1, step_rows, width)
+        if 0 in parts:
+            dst[first] = mm(latents[half, :k_rows], grads[1, :, cols])
+        if 1 in parts:
+            rest = mm(latents[half, k_rows:], grads[0, :, cols])
+            dst[first + 1 : first + chunks] = rest.reshape(chunks - 1, step_rows, width)
 
     step_rows = k_rows
     chunks = tall // step_rows
@@ -216,9 +213,12 @@
     def home(chunk):
         return 2 * group + (1 if chunk else 0)
 
+    def landed(slot, chunk):
+        return fin_r.at[slot, max(chunk - 1, 0)]
+
     def final_copy(source, spot, slot, chunk, sent, to):
         return copy(
-            source.at[at(spot, chunk)], fin.at[slot, chunk, core], sent, fin_r.at[slot, chunk],
+            source.at[at(spot, chunk)], fin.at[slot, chunk, core], sent, landed(slot, chunk),
             (to, home(chunk)),
         )
 
@@ -245,9 +245,11 @@
         for chunk in which:
             near_copy(spot, chunk).start()
 
-    term(near_send, 0, order[0], 1 - inner)
+    term(near_send, 0, order[0], 1 - inner, (0,))
     pl.semaphore_wait(barrier, entered)
-    send_near(0, spans[0])
+    send_near(0, spans[0][:1])
+    term(near_send, 0, order[0], 1 - inner, (1,))
+    send_near(0, spans[0][1:])
     if line:
         term(near_send, 1, order[1], 1 - inner)
         raw_copy().start()
@@ -327,7 +329,7 @@
 
     def arrived(slot, chunk):
         ref = fin.at[slot, chunk]
-        copy(ref, ref, fs_s, fin_r.at[slot, chunk], partner_core).wait_recv()
+        copy(ref, ref, fs_s, landed(slot, chunk), partner_core).wait_recv()
         return fin[slot, chunk]
 
     def pass_on(spot):
@@ -378,7 +380,7 @@
         else:
             km_out[0] = mine
             back_send[chunk] = other
-        return gram_pair(jnp.concatenate([mine, other], axis=0))
+        return gram(jnp.concatenate([mine, other], axis=0))
 
     for which, members in enumerate((range(1), range(1, chunks))):
 
@@ -397,9 +399,9 @@
             pair = complete(which, members[0])
             for chunk in members[1:]:
                 pair = pair + complete(which, chunk)
-            row_send[...] = fold(gram_of(pair))
-
-    for step in range(1, 2 * n_group):
+            row_send[...] = fold(pair)
+
+    for step in reversed(range(1, 2 * n_group)):
         each = copy(
             row_send, row_recv.at[step - 1], y_s, y_r, owner(step)
         )
@@ -563,7 +565,7 @@
             vmem((2 * n_group - 1,) + folded, F32),
             vmem((2,) + square, F32),
             dma, dma(((n_outer - 1) * chunks,)),
-            dma, dma((n_outer, chunks)), dma((chunks,)), dma,
+            dma, dma((n_outer, chunks - 1)), dma((chunks,)), dma,
             dma, dma, dma, dma, dma, dma, dma, dma, dma, dma,
             dma, dma((2,)),
         ],

time: 26.8 us -> 26.3 us (0.981)
  Pallas kernels: 26 us -> 25.5 us
    pallas_call x1, Pallas kernels: 25.1 us -> 24.6 us  [local(): pl.pallas_call(functools.partial(kernel, n_dp, n_mp, heads), out_shape=[v...]
where the time goes in v6:
time: 26.3 us; the launch traced here: 26.1 us
  Pallas kernels  25.5 us (97%)
  between operations  0.64 us (2%)
    pallas_call x1, Pallas kernels, local(): pl.pallas_call(functools.partial(kernel, n_dp, n_mp, heads), out_shape=[v...  24.6 us
    pallas_call x1, Pallas kernels, local(): pl.pallas_call(functools.partial(finish, n_mp), out_shape=[jax.ShapeDtype...  0.89 us

profile of v6, /device:TPU:0, one launch (start us, length us, event | category | flops | bytes accessed | tf_op | source)
XLA Modules:
  0.0 26.1 jit_solution(2808623279828195851)
XLA Ops:
  0.6 24.6 %shard_map.147 = (f32[1,192,128]{2,1,0:T(8,128)S(1)}, f32[1,64,128]{2,1,0:T(8,128)S(1)}, f32[1,192,128]{2,1,0:T(8,128)S(1)}, f32[1,64,128]{2,1,0:T(8,128)S(1)}, ...) custom-call(bf16[2,192,256]{2,1,0:T(8,128)(2,1)} %bitcast.4, ...), custom_call_target="tpu_custom_call" | custom-call | tf_op jit(solution)/shard_map/pallas_call | solution.py:544
  25.2 0.9 %shard_map.148 = (f32[1,192,128]{2,1,0:T(8,128)}, f32[1,64,128]{2,1,0:T(8,128)}, f32[1,192,128]{2,1,0:T(8,128)}, f32[1,64,128]{2,1,0:T(8,128)}) custom-call(f32[1,192,128]{2,1,0:T(8,128)S(1)} %get-tuple-element.12.qw_ref, f32[1,64,128]{2,1,0:T(8,128)S(1)} %get-tuple-element.13.kw_ref, f32[1,192,128]{2,1,0:T(8,128)S(1)} %get-tuple-element.14.qm_ref, ...), custom_call_target="tpu_custom_call" | custom-call | tf_op jit(solution)/shard_map/pallas_call | solution.py:576

commit v7 on v6

--- a/solution.py
+++ b/solution.py
@@ -144,21 +144,26 @@
             pltpu.make_async_copy(ref, ref, in_sems.at[i]).wait()
 
     barrier = pltpu.get_barrier_semaphore()
-    for step in range(1, n_dp):
-        for column in (mp, other_core):
-            pl.semaphore_signal(
-                barrier, inc=1, device_id=(lax.rem(dp + step, n_dp), column), device_id_type=MESH
-            )
+
+    def greet(*where):
+        pl.semaphore_signal(barrier, inc=1, device_id=where, device_id_type=MESH)
+
     def owner(step):
         across = lax.rem(dp + (step // n_group) * heads, n_dp)
         return across, 2 * lax.rem(group + step, n_group) + core
 
-    for step in range(n_group + 1, 2 * n_group):
-        pl.semaphore_signal(barrier, inc=1, device_id=owner(step), device_id_type=MESH)
+    across_x = dp + 1 - 2 * inner
+    by = [partner(outer, n_outer, step) for step in range(n_outer)]
+    for step in range(n_outer - 1, 0, -1):
+        greet(2 * by[step] + inner, mp)
+        greet(2 * by[step] + inner, other_core)
+        greet(2 * by[step] + 1 - inner, mp)
+    greet(across_x, mp)
+    greet(across_x, other_core)
+    for step in range(2 * n_group - 1, n_group, -1):
+        greet(*owner(step))
     for step in range(1, n_mp):
-        pl.semaphore_signal(
-            barrier, inc=1, device_id=(dp, lax.rem(mp + step, n_mp)), device_id_type=MESH
-        )
+        greet(dp, lax.rem(mp + step, n_mp))
 
     def copy(src, dst, send, recv, where):
         return pltpu.make_async_remote_copy(
@@ -184,14 +189,12 @@
     step_rows = k_rows
     chunks = tall // step_rows
     loaded(0, 1)
-    entered = 2 * (n_dp - 1) + (n_mp - 1) + (n_group - 1)
-    across_x = dp + 1 - 2 * inner
+    entered = 3 * (n_outer - 1) + 2 + (n_mp - 1) + (n_group - 1)
     neighbour = (across_x, mp)
     partner_core = (dp, other_core)
     last = n_outer - 1
     line = n_outer == 4
     inside = lax.rem(lax.div(outer, 2) + lax.rem(outer, 2), 2)
-    by = [partner(outer, n_outer, step) for step in range(n_outer)]
 
     def at(spot, chunk):
         return spot * chunks + chunk
@@ -213,8 +216,10 @@
     def home(chunk):
         return 2 * group + (1 if chunk else 0)
 
+    fine_slot = 2 if line else n_outer
+
     def landed(slot, chunk):
-        return fin_r.at[slot, max(chunk - 1, 0)]
+        return fin_r.at[n_outer + max(chunk - 1, 0) if slot == fine_slot else slot]
 
     def final_copy(source, spot, slot, chunk, sent, to):
         return copy(
@@ -235,11 +240,16 @@
             (2 * by[1] + inner, mp),
         )
 
-    def raw_copy():
+    def raw_copy(first):
+        count = chunks - first
         return copy(
-            near_send.at[pl.ds(at(1, kept), chunks - kept)], raw_recv, fs_s, rw_r,
-            (2 * split_to + inner, mp),
-        )
+            near_send.at[pl.ds(at(1, first), count)], raw_recv.at[pl.ds(first, count)],
+            fs_s, rw_r, (2 * split_to + inner, mp),
+        )
+
+    def by_role(act):
+        for held in range(2):
+            pl.when(inside == held)(functools.partial(act, held))
 
     def send_near(spot, which):
         for chunk in which:
@@ -252,13 +262,17 @@
     send_near(0, spans[0][1:])
     if line:
         term(near_send, 1, order[1], 1 - inner)
-        raw_copy().start()
+        by_role(lambda held: raw_copy(0 if held else kept).start())
         term(own, 1, order[1], inner)
-        for chunk in range(kept, chunks):
-            far_copy(1, chunk, split_to).start()
+
+        def send_split(held):
+            for chunk in range(0 if held else kept, chunks):
+                far_copy(1, chunk, split_to).start()
+            if not held:
+                send_near(1, range(kept))
+
+        by_role(send_split)
         term(near_send, 2, order[2], 1 - inner)
-
-        send_near(1, spans[1])
         send_near(2, spans[2])
 
     loaded(2, 3)
@@ -285,7 +299,7 @@
 
     if line:
         term(near_send, last, order[last], 1 - inner)
-        send_last(range(kept))
+        by_role(lambda held: send_last(range(kept)) if held else None)
     else:
         for spot in range(1, n_outer):
             term(near_send, spot, order[spot], 1 - inner)
@@ -327,10 +341,10 @@
         where = at(spot, chunk)
         own[where] = own[where] + near_recv[where]
 
-    def arrived(slot, chunk):
-        ref = fin.at[slot, chunk]
-        copy(ref, ref, fs_s, landed(slot, chunk), partner_core).wait_recv()
-        return fin[slot, chunk]
+    def arrived(slot, members):
+        ref = fin.at[slot, pl.ds(members[0], len(members))]
+        sem = landed(slot, members[0])
+        copy(ref, ref, fs_s, sem, partner_core).wait_recv()
 
     def pass_on(spot):
         for chunk in spans[spot]:
@@ -345,11 +359,13 @@
                     far_copy(0, chunk, by[3]).start()
                 else:
                     relay_copy(chunk).start()
-            pass_on(1)
-            raw_copy().wait_recv()
-            low = pl.ds(at(last, kept), chunks - kept)
-            near_send[low] = near_send[low] + raw_recv[...]
-            send_last(range(kept, chunks))
+            if not held:
+                pass_on(1)
+            first = kept if held else 0
+            raw_copy(first).wait_recv()
+            part = pl.ds(at(last, first), chunks - first)
+            near_send[part] = near_send[part] + raw_recv[pl.ds(first, chunks - first)]
+            send_last(range(first, chunks))
             for chunk in spans[2]:
                 if held:
                     relay_copy(chunk).wait_recv()
@@ -357,18 +373,16 @@
                 meet(2, chunk)
                 far_copy(2, chunk, whole_to).start()
 
-        for held in range(2):
-
-            @pl.when(inside == held)
-            def _():
-                forward(held)
+        by_role(forward)
 
     else:
         for spot in range(last):
             pass_on(spot)
 
     def complete(which, chunk):
-        added = [arrived(slot, chunk) for slot in ((1, 2, last) if line else range(n_outer))]
+        if line:
+            arrived(2, range(chunk, chunk + 1))
+        added = [fin[slot, chunk] for slot in range(1 if line else 0, n_outer)]
         mine = own[at(last, chunk)]
         other = base[chunk]
         for each in added:
@@ -391,11 +405,14 @@
 
                 @pl.when(inside == 1)
                 def _():
+                    arrived(0, members)
                     for chunk in members:
-                        early = arrived(0, chunk)
+                        early = fin[0, chunk]
                         own[at(last, chunk)] = own[at(last, chunk)] + early[which]
                         base[chunk] = base[chunk] + early[1 - which]
 
+            for slot in (1, last) if line else range(n_outer):
+                arrived(slot, members)
             pair = complete(which, members[0])
             for chunk in members[1:]:
                 pair = pair + complete(which, chunk)
@@ -470,24 +487,33 @@
     shrink_out[...] = jnp.broadcast_to(shrink, shrink_out.shape)
     qw_out[0] = (state[0, k_rows:] * keep) * shrink
     kw_out[0] = (state[0, :k_rows] * keep) * shrink
+    def drain(sent, passed):
+        for count, ref, sem in ((sent, near_send, ns_s), (passed, own, fs_s)):
+            part = ref.at[pl.ds(0, count)]
+            copy(part, part, sem, sem, partner_core).wait_send()
+
+    if line:
+        by_role(
+            lambda held: drain(
+                last * chunks + (0 if held else kept), last * chunks + (chunks if held else kept)
+            )
+        )
+    else:
+        drain(n_outer * chunks, last * chunks)
+    for each in (all_peaks, all_peaks2, all_rows):
+        each.wait_send()
+    for which in range(2):
+
+        @on_core(which)
+        def _():
+            base_copy(which).wait_send()
+            back_copy(which).wait_send()
+
     swap2[0].wait_recv()
     for which, (moment, part_out) in enumerate(((qm_out, qy_out), (km_out, ky_out))):
         part_out[0] = mm3(split(moment[0]), split(mix[which]))
     swap2[1].wait_recv()
-    sent = sum(len(span) for span in spans)
-    passed = sent - len(spans[last]) + (2 * (chunks - kept) if line else 0)
-    for count, ref, sem in ((sent, near_send, ns_s), (passed, own, fs_s)):
-        part = ref.at[pl.ds(0, count)]
-        copy(part, part, sem, sem, (dp, other_core)).wait_send()
     copy(mix, mix, m_s, m_s, (dp, other_core)).wait_send()
-    for each in (all_peaks, all_peaks2, all_rows):
-        each.wait_send()
-    for which in range(2):
-
-        @on_core(which)
-        def _():
-            base_copy(which).wait_send()
-            back_copy(which).wait_send()
 
 
 def finish(
@@ -554,7 +580,7 @@
             vmem((2, rows, width), F32),
             dma((5,)),
             blocks(n_outer * chunks), blocks((n_outer - 1) * chunks), blocks(n_outer * chunks),
-            blocks(chunks), blocks(chunks - chunks // 2),
+            blocks(chunks), blocks(chunks),
             vmem((n_outer, chunks, 2, k_rows, width), F32),
             blocks(chunks), blocks(chunks - 1), blocks(chunks - 1),
             vmem(tile, F32),
@@ -565,7 +591,7 @@
             vmem((2 * n_group - 1,) + folded, F32),
             vmem((2,) + square, F32),
             dma, dma(((n_outer - 1) * chunks,)),
-            dma, dma((n_outer, chunks - 1)), dma((chunks,)), dma,
+            dma, dma((n_outer + (chunks - 1 if n_outer == 4 else 0),)), dma((chunks,)), dma,
             dma, dma, dma, dma, dma, dma, dma, dma, dma, dma,
             dma, dma((2,)),
         ],

time: 26.3 us -> 26.2 us (level)
  no operation moved by 1% of the time
where the time goes in v7:
time: 26.2 us; the launch traced here: 26.1 us
  Pallas kernels  25.4 us (97%)
  between operations  0.64 us (2%)
    pallas_call x1, Pallas kernels, local(): pl.pallas_call(functools.partial(kernel, n_dp, n_mp, heads), out_shape=[v...  24.5 us
    pallas_call x1, Pallas kernels, local(): pl.pallas_call(functools.partial(finish, n_mp), out_shape=[jax.ShapeDtype...  0.89 us

profile of v7, /device:TPU:0, one launch (start us, length us, event | category | flops | bytes accessed | tf_op | source)
XLA Modules:
  0.0 26.1 jit_solution(11360192638292038853)
XLA Ops:
  0.6 24.5 %shard_map.147 = (f32[1,192,128]{2,1,0:T(8,128)S(1)}, f32[1,64,128]{2,1,0:T(8,128)S(1)}, f32[1,192,128]{2,1,0:T(8,128)S(1)}, f32[1,64,128]{2,1,0:T(8,128)S(1)}, ...) custom-call(bf16[2,192,256]{2,1,0:T(8,128)(2,1)} %bitcast.4, ...), custom_call_target="tpu_custom_call" | custom-call | tf_op jit(solution)/shard_map/pallas_call | solution.py:570
  25.2 0.9 %shard_map.148 = (f32[1,192,128]{2,1,0:T(8,128)}, f32[1,64,128]{2,1,0:T(8,128)}, f32[1,192,128]{2,1,0:T(8,128)}, f32[1,64,128]{2,1,0:T(8,128)}) custom-call(f32[1,192,128]{2,1,0:T(8,128)S(1)} %get-tuple-element.12.qw_ref, f32[1,64,128]{2,1,0:T(8,128)S(1)} %get-tuple-element.13.kw_ref, f32[1,192,128]{2,1,0:T(8,128)S(1)} %get-tuple-element.14.qm_ref, ...), custom_call_target="tpu_custom_call" | custom-call | tf_op jit(solution)/shard_map/pallas_call | solution.py:602

commit v8 on v7

--- a/solution.py
+++ b/solution.py
@@ -450,15 +450,21 @@
         km_out[0] = back_recv[0]
 
     all_rows.wait_recv()
-    whole = unfold(row_send[...] + jnp.sum(row_recv[...], axis=0))
+    folded = row_send[...] + jnp.sum(row_recv[...], axis=0)
+    whole = unfold(folded)
+    raw = split(whole)
+    raw_square = mm_deep(raw, raw)
 
     eye = (
         lax.broadcasted_iota(jnp.int32, (width, width), 0)
         == lax.broadcasted_iota(jnp.int32, (width, width), 1)
     ).astype(F32)
-    trace = jnp.sum(jnp.sum(whole * eye, axis=0, keepdims=True), axis=1, keepdims=True)
+    top = width // 2
+    diagonal = jnp.sum(folded[:top] * eye[:top], axis=0, keepdims=True) + folded[top:]
+    trace = jnp.sum(diagonal, axis=1, keepdims=True)
     scale = 1.0 / jnp.sqrt(trace + 1.0)
-    current = whole * (scale * scale)
+    shift = scale * scale
+    current = whole * shift
     mixed = None
     swap2 = [
         copy(ref.at[1 - core], ref.at[1 - core], m_s, m_r.at[i], (dp, other_core))
@@ -466,7 +472,7 @@
     ]
     for step in range(ITERS):
         parts = split(current)
-        square = mm_deep(parts, parts)
+        square = mm_deep(parts, parts) if step else raw_square * (shift * shift)
         poly = COEFF_A * eye + COEFF_B * current + COEFF_C * square
         if step + 1 == ITERS:
             break

time: 26.2 us -> 26.1 us (level)
  no operation moved by 1% of the time
where the time goes in v8:
time: 26.1 us; the launch traced here: 25.9 us
  Pallas kernels  25.3 us (97%)
  between operations  0.64 us (2%)
    pallas_call x1, Pallas kernels, local(): pl.pallas_call(functools.partial(kernel, n_dp, n_mp, heads), out_shape=[v...  24.4 us
    pallas_call x1, Pallas kernels, local(): pl.pallas_call(functools.partial(finish, n_mp), out_shape=[jax.ShapeDtype...  0.89 us

profile of v8, /device:TPU:0, one launch (start us, length us, event | category | flops | bytes accessed | tf_op | source)
XLA Modules:
  0.0 25.9 jit_solution(989257422394647905)
XLA Ops:
  0.6 24.4 %shard_map.147 = (f32[1,192,128]{2,1,0:T(8,128)S(1)}, f32[1,64,128]{2,1,0:T(8,128)S(1)}, f32[1,192,128]{2,1,0:T(8,128)S(1)}, f32[1,64,128]{2,1,0:T(8,128)S(1)}, ...) custom-call(bf16[2,192,256]{2,1,0:T(8,128)(2,1)} %bitcast.4, ...), custom_call_target="tpu_custom_call" | custom-call | tf_op jit(solution)/shard_map/pallas_call | solution.py:576
  25.1 0.9 %shard_map.148 = (f32[1,192,128]{2,1,0:T(8,128)}, f32[1,64,128]{2,1,0:T(8,128)}, f32[1,192,128]{2,1,0:T(8,128)}, f32[1,64,128]{2,1,0:T(8,128)}) custom-call(f32[1,192,128]{2,1,0:T(8,128)S(1)} %get-tuple-element.12.qw_ref, f32[1,64,128]{2,1,0:T(8,128)S(1)} %get-tuple-element.13.kw_ref, f32[1,192,128]{2,1,0:T(8,128)S(1)} %get-tuple-element.14.qm_ref, ...), custom_call_target="tpu_custom_call" | custom-call | tf_op jit(solution)/shard_map/pallas_call | solution.py:608

commit v9 on v8

--- a/solution.py
+++ b/solution.py
@@ -359,13 +359,13 @@
                     far_copy(0, chunk, by[3]).start()
                 else:
                     relay_copy(chunk).start()
-            if not held:
-                pass_on(1)
             first = kept if held else 0
             raw_copy(first).wait_recv()
             part = pl.ds(at(last, first), chunks - first)
             near_send[part] = near_send[part] + raw_recv[pl.ds(first, chunks - first)]
             send_last(range(first, chunks))
+            if not held:
+                pass_on(1)
             for chunk in spans[2]:
                 if held:
                     relay_copy(chunk).wait_recv()

time: 26.1 us -> 26.1 us (level)
  no operation moved by 1% of the time
where the time goes in v9:
time: 26.1 us; the launch traced here: 25.9 us
  Pallas kernels  25.3 us (97%)
  between operations  0.64 us (2%)
    pallas_call x1, Pallas kernels, local(): pl.pallas_call(functools.partial(kernel, n_dp, n_mp, heads), out_shape=[v...  24.4 us
    pallas_call x1, Pallas kernels, local(): pl.pallas_call(functools.partial(finish, n_mp), out_shape=[jax.ShapeDtype...  0.89 us

profile of v9, /device:TPU:0, one launch (start us, length us, event | category | flops | bytes accessed | tf_op | source)
XLA Modules:
  0.0 25.9 jit_solution(13241014167199834494)
XLA Ops:
  0.6 24.4 %shard_map.147 = (f32[1,192,128]{2,1,0:T(8,128)S(1)}, f32[1,64,128]{2,1,0:T(8,128)S(1)}, f32[1,192,128]{2,1,0:T(8,128)S(1)}, f32[1,64,128]{2,1,0:T(8,128)S(1)}, ...) custom-call(bf16[2,192,256]{2,1,0:T(8,128)(2,1)} %bitcast.4, ...), custom_call_target="tpu_custom_call" | custom-call | tf_op jit(solution)/shard_map/pallas_call | solution.py:576
  25.1 0.9 %shard_map.148 = (f32[1,192,128]{2,1,0:T(8,128)}, f32[1,64,128]{2,1,0:T(8,128)}, f32[1,192,128]{2,1,0:T(8,128)}, f32[1,64,128]{2,1,0:T(8,128)}) custom-call(f32[1,192,128]{2,1,0:T(8,128)S(1)} %get-tuple-element.12.qw_ref, f32[1,64,128]{2,1,0:T(8,128)S(1)} %get-tuple-element.13.kw_ref, f32[1,192,128]{2,1,0:T(8,128)S(1)} %get-tuple-element.14.qm_ref, ...), custom_call_target="tpu_custom_call" | custom-call | tf_op jit(solution)/shard_map/pallas_call | solution.py:608
